TPU v7x, 8 devices: a whole 2x2x1 slice. The times are simulated.
8 devices in a mesh: tp: 4 (over z, y, x), cp: 2 (over core).
Axes of the slice: x: 2, y: 2, z: 1, core: 2. Of those that a mesh axis runs over, the one named last changes fastest.
Arguments:
- tokens: int32 [2048], P('cp')
- pos: int32 [2048], P('cp')
- doc_id: int32 [2048], P('cp')
- dy: bfloat16 [2048, 2048], P('cp')
- table: bfloat16 [32000, 2048], P('tp')
- w_q: bfloat16 [2048, 2048], P(None, 'tp')
- w_k: bfloat16 [2048, 2048], P(None, 'tp')
- w_v: bfloat16 [2048, 2048], P(None, 'tp')
- w_o: bfloat16 [2048, 2048], P('tp')
- w_gate: bfloat16 [2048, 5504], P(None, 'tp')
- w_up: bfloat16 [2048, 5504], P(None, 'tp')
- w_down: bfloat16 [5504, 2048], P('tp')
- gain_one: bfloat16 [2048], replicated
- gain_two: bfloat16 [2048], replicated
- inv_freq: float32 [64], replicated
Outputs:
- output 1: bfloat16 [2048, 2048], P('cp')
- output 2: float32 [32000, 2048], P('tp')
- output 3: float32 [2048, 2048], P(None, 'tp')
- output 4: float32 [2048, 2048], P(None, 'tp')
- output 5: float32 [2048, 2048], P(None, 'tp')
- output 6: float32 [2048, 2048], P('tp')
- output 7: float32 [2048, 5504], P(None, 'tp')
- output 8: float32 [2048, 5504], P(None, 'tp')
- output 9: float32 [5504, 2048], P('tp')
- output 10: float32 [2048], replicated
- output 11: float32 [2048], replicated
All inputs are finite; a program needn't handle non-finite values.
Results may differ from a plain program's by a relative error of at most 0.0147216.
Values are sent between devices in bfloat16 or wider.
A program may use at most 1 GiB of HBM per device.

v0:
```python
import jax
import jax.numpy as jnp
from jax import lax
from jax.sharding import PartitionSpec as P

NORM_EPS = 1e-5
NEG_BIG = -1e30


def rms_stats(feats):
    inv_rms = lax.rsqrt(jnp.mean(feats * feats, axis=-1, keepdims=True) + NORM_EPS)
    return feats * inv_rms, inv_rms


def rms_back(d_normed, normed, inv_rms):
    return inv_rms * (d_normed - normed * jnp.mean(d_normed * normed, axis=-1, keepdims=True))


def rotate(tensor_in, cosine, sine):
    half = tensor_in.shape[-1] // 2
    first = tensor_in[..., :half]
    second = tensor_in[..., half:]
    return jnp.concatenate([first * cosine - second * sine, second * cosine + first * sine], axis=-1)


def to_bf16(feats):
    return feats.astype(jnp.bfloat16).astype(jnp.float32)


def slot_sequence(slot, block_len, cp_count):
    shard = slot // (2 * block_len)
    within = slot % (2 * block_len)
    block_no = jnp.where(within < block_len, shard, 2 * cp_count - 1 - shard)
    return block_no * block_len + within % block_len


def solution(mesh):
    cp_count = mesh.shape["cp"]

    def device_step(tokens, pos, doc_id, dy, table, w_q, w_k, w_v, w_o, w_gate, w_up, w_down, gain_one, gain_two, inv_freq):
        span = tokens.shape[0]
        total = span * cp_count
        rows = table.shape[0]
        head_dim = 2 * inv_freq.shape[0]
        kv_local = w_k.shape[1] // head_dim
        q_local = w_q.shape[1] // head_dim
        group = q_local // kv_local
        scale = head_dim ** -0.5
        tp_rank = lax.axis_index("tp")
        cp_rank = lax.axis_index("cp")
        gain_a = gain_one.astype(jnp.float32)
        gain_b = gain_two.astype(jnp.float32)

        local_ids = tokens - tp_rank * rows
        owned = (local_ids >= 0) & (local_ids < rows)
        safe_ids = jnp.where(owned, local_ids, 0)
        picked = jnp.where(owned[:, None], jnp.take(table, safe_ids, axis=0), jnp.zeros((), jnp.bfloat16))
        embed = lax.psum(picked, "tp").astype(jnp.float32)

        normed_a, inv_a = rms_stats(embed)
        act_a = (normed_a * gain_a).astype(jnp.bfloat16)
        angle = pos.astype(jnp.float32)[:, None, None] * inv_freq
        cosine = jnp.cos(angle)
        sine = jnp.sin(angle)
        query = jnp.dot(act_a, w_q, preferred_element_type=jnp.float32).reshape(span, q_local, head_dim)
        query = rotate(query, cosine, sine).astype(jnp.bfloat16).reshape(span, kv_local, group, head_dim)
        key_loc = jnp.dot(act_a, w_k, preferred_element_type=jnp.float32).reshape(span, kv_local, head_dim)
        key_loc = rotate(key_loc, cosine, sine).astype(jnp.bfloat16)
        value_loc = jnp.dot(act_a, w_v, preferred_element_type=jnp.float32).astype(jnp.bfloat16).reshape(span, kv_local, head_dim)

        key_all = lax.all_gather(key_loc, "cp", axis=0, tiled=True)
        value_all = lax.all_gather(value_loc, "cp", axis=0, tiled=True)
        doc_all = lax.all_gather(doc_id, "cp", axis=0, tiled=True)
        q_seq = slot_sequence(cp_rank * span + jnp.arange(span), span // 2, cp_count)
        k_seq = slot_sequence(jnp.arange(total), span // 2, cp_count)
        allowed = (doc_id[:, None] == doc_all[None, :]) & (k_seq[None, :] <= q_seq[:, None])

        scores = jnp.einsum("qkgd,skd->kgqs", query, key_all, preferred_element_type=jnp.float32) * scale
        attn_prob = jax.nn.softmax(jnp.where(allowed, scores, NEG_BIG), axis=-1)
        prob_b = attn_prob.astype(jnp.bfloat16)
        attended = jnp.einsum("kgqs,skd->qkgd", prob_b, value_all, preferred_element_type=jnp.float32)
        attended = attended.astype(jnp.bfloat16).reshape(span, q_local * head_dim)
        residual = embed + lax.psum(jnp.dot(attended, w_o, preferred_element_type=jnp.float32), "tp")
        normed_b, inv_b = rms_stats(residual)
        act_b = (normed_b * gain_b).astype(jnp.bfloat16)
        gate = jnp.dot(act_b, w_gate, preferred_element_type=jnp.float32)
        up_val = jnp.dot(act_b, w_up, preferred_element_type=jnp.float32)
        gate_sig = jax.nn.sigmoid(gate)
        hidden = (gate * gate_sig * up_val).astype(jnp.bfloat16)
        layer_out = residual + lax.psum(jnp.dot(hidden, w_down, preferred_element_type=jnp.float32), "tp")

        grad_down = jnp.einsum("tf,td->fd", hidden, dy, preferred_element_type=jnp.float32)
        d_hidden = to_bf16(jnp.einsum("td,fd->tf", dy, w_down, preferred_element_type=jnp.float32))
        d_gate = (d_hidden * up_val * gate_sig * (1.0 + gate * (1.0 - gate_sig))).astype(jnp.bfloat16)
        d_up = (d_hidden * gate * gate_sig).astype(jnp.bfloat16)
        grad_gate = jnp.einsum("td,tf->df", act_b, d_gate, preferred_element_type=jnp.float32)
        grad_up = jnp.einsum("td,tf->df", act_b, d_up, preferred_element_type=jnp.float32)
        d_act_b = jnp.einsum("tf,df->td", d_gate, w_gate, preferred_element_type=jnp.float32)
        d_act_b = d_act_b + jnp.einsum("tf,df->td", d_up, w_up, preferred_element_type=jnp.float32)
        d_act_b = to_bf16(lax.psum(d_act_b, "tp"))
        grad_gain_b = jnp.sum(d_act_b * normed_b, axis=0)
        d_resid = dy.astype(jnp.float32) + rms_back(d_act_b * gain_b, normed_b, inv_b)
        d_resid_b = d_resid.astype(jnp.bfloat16)
        grad_out = jnp.einsum("tc,td->cd", attended, d_resid_b, preferred_element_type=jnp.float32)
        d_att = jnp.einsum("td,cd->tc", d_resid_b, w_o, preferred_element_type=jnp.float32)
        d_att = d_att.astype(jnp.bfloat16).reshape(span, kv_local, group, head_dim)
        d_prob = to_bf16(jnp.einsum("qkgd,skd->kgqs", d_att, value_all, preferred_element_type=jnp.float32))
        d_scores = attn_prob * (d_prob - jnp.sum(attn_prob * d_prob, axis=-1, keepdims=True))
        d_scores = (d_scores * scale).astype(jnp.bfloat16)
        d_query = jnp.einsum("kgqs,skd->qkgd", d_scores, key_all, preferred_element_type=jnp.float32)
        d_key_all = jnp.einsum("kgqs,qkgd->skd", d_scores, query, preferred_element_type=jnp.float32)
        d_value_all = jnp.einsum("kgqs,qkgd->skd", prob_b, d_att, preferred_element_type=jnp.float32)
        d_key = lax.psum_scatter(d_key_all, "cp", scatter_dimension=0, tiled=True)
        d_value = lax.psum_scatter(d_value_all, "cp", scatter_dimension=0, tiled=True)
        d_q_pre = rotate(to_bf16(d_query).reshape(span, q_local, head_dim), cosine, -sine)
        d_q_pre = d_q_pre.astype(jnp.bfloat16).reshape(span, q_local * head_dim)
        d_k_pre = rotate(to_bf16(d_key), cosine, -sine).astype(jnp.bfloat16).reshape(span, kv_local * head_dim)
        d_v_pre = d_value.astype(jnp.bfloat16).reshape(span, kv_local * head_dim)
        grad_q = jnp.einsum("td,tc->dc", act_a, d_q_pre, preferred_element_type=jnp.float32)
        grad_k = jnp.einsum("td,tc->dc", act_a, d_k_pre, preferred_element_type=jnp.float32)
        grad_v = jnp.einsum("td,tc->dc", act_a, d_v_pre, preferred_element_type=jnp.float32)
        d_act_a = jnp.einsum("tc,dc->td", d_q_pre, w_q, preferred_element_type=jnp.float32)
        d_act_a = d_act_a + jnp.einsum("tc,dc->td", d_k_pre, w_k, preferred_element_type=jnp.float32)
        d_act_a = d_act_a + jnp.einsum("tc,dc->td", d_v_pre, w_v, preferred_element_type=jnp.float32)
        d_act_a = to_bf16(lax.psum(d_act_a, "tp"))
        grad_gain_a = jnp.sum(d_act_a * normed_a, axis=0)
        d_embed = d_resid + rms_back(d_act_a * gain_a, normed_a, inv_a)
        table_part = jax.ops.segment_sum(jnp.where(owned[:, None], d_embed, 0.0), safe_ids, num_segments=rows)
        grad_table = lax.psum(table_part, "cp")
        weight_grads = lax.psum((grad_q, grad_k, grad_v, grad_out, grad_gate, grad_up, grad_down, grad_gain_a, grad_gain_b), "cp")
        return (layer_out.astype(jnp.bfloat16), grad_table) + tuple(weight_grads)

    col_spec = P(None, "tp")
    row_spec = P("tp", None)
    tok_spec = P("cp")
    rep_spec = P(None)
    in_specs = (tok_spec, tok_spec, tok_spec, P("cp", None), row_spec, col_spec, col_spec, col_spec, row_spec, col_spec, col_spec, row_spec, rep_spec, rep_spec, rep_spec)
    out_specs = (P("cp", None), row_spec, col_spec, col_spec, col_spec, row_spec, col_spec, col_spec, row_spec, rep_spec, rep_spec)
    return jax.shard_map(device_step, mesh=mesh, in_specs=in_specs, out_specs=out_specs, check_vma=False)
```

profile of v0, /device:TPU:0, one launch (start us, length us, event | category | flops | bytes accessed | tf_op | source)
XLA Modules:
  0.0 1820.8 jit_solution(2898189783651721753)
XLA Ops:
  8.7 34.6 %gather_fusion = bf16[1024,2048]{1,0:T(8,128)(2,1)} fusion(bf16[8000,2048]{1,0:T(8,128)(2,1)} %param.19, s32[1024]{0:T(1024)S(1)} %fusion.79), kind=kCustom, calls=%fused_computation | custom fusion | bytes 8392704 | tf_op jit(solution)/shard_map/jit(_take)/gather | solution.py:57
  50.5 109.2 %all-reduce.9.cloned.1.call-done = bf16[1024,2048]{1,0:T(8,128)(2,1)} async-done(((bf16[1024,2048]{1,0:T(8,128)(2,1)}), bf16[1024,2048]{1,0:T(8,128)(2,1)}) %all-reduce.9.cloned.1.call-update) | async-done | bytes 4194320 | tf_op jit(solution)/shard_map/psum | solution.py:58
  208.6 17.2 fusion.11
  225.8 14.4 fusion.10
  240.2 17.8 fusion.54
  265.8 10.4 convolution_convert_fusion.1
  276.1 149.5 %all-reduce.11.cloned.1.call-done = f32[1024,2048]{1,0:T(8,128)} async-done(((f32[1024,2048]{1,0:T(8,128)}), f32[1024,2048]{1,0:T(8,128)}) %all-reduce.11.cloned.1.call-update) | async-done | bytes 8388624 | tf_op jit(solution)/shard_map/psum | solution.py:83
  434.8 11.4 fusion.101
  446.2 13.4 fusion.41
  461.2 9.4 fusion.102
  470.6 10.0 fusion.103
  480.6 13.0 convolution_add_fusion
  493.6 392.8 %all-reduce.16 = bf16[1024,2048]{1,0:T(8,128)(2,1)} all-reduce(f32[1024,2048]{1,0:T(8,128)} %convolution_add_fusion), channel_id=1, replica_groups=mesh['tp'=4,'cp'=2] {'tp'}, use_global_device_ids=true, to_apply=%region_7.8 | all-reduce | flops 2097152 | bytes 12582912 | tf_op jit(solution)/shard_map/psum | solution.py:100
  892.9 12.4 fusion.30
  910.6 21.6 %fusion.3 = (f32[4,1024]{1,0:T(4,128)S(1)}, bf16[4,2048,1024]{2,1,0:T(8,128)(2,1)}) fusion(f32[4,1024]{1,0:T(4,128)S(1)} %fusion.10, f32[4,1024]{1,0:T(4,128)S(1)} %get-tuple-element.55, f32[4,2048,1024]{2,1,0:T(8,128)} %get-tuple-element.56, pred[1024,2048]{0,1:T(8,128)(4,1)S(1)} %copy-done.8, bf16[2048,4,128]{0,2,1:T(8,128)(2,1)S(1)} %copy-done.38, ...), kind=kOutput, calls=%fused_computation.7 | convolution fusion | flops 2214588416 | bytes 55623680 | tf_op jit(solution)/shard_map/qkgd,skd->kgqs/dot_general | solution.py:107
  932.2 25.7 %fusion.12 = bf16[4,1024,2048]{1,2,0:T(8,128)(2,1)} fusion(bf16[4,2048,1024]{2,1,0:T(8,128)(2,1)} %get-tuple-element.58, f32[4,1024]{1,0:T(4,128)S(1)} %get-tuple-element.57, f32[4,1024]{1,0:T(4,128)S(1)} %fusion.10, f32[4,1024]{1,0:T(4,128)S(1)} %get-tuple-element.55, f32[4,2048,1024]{2,1,0:T(8,128)} %get-tuple-element.56, pred[1024,2048]{0,1:T(8,128)(4,1)S(1)} %copy-done.8), kind=kLoop, calls=%fused_computation.17 | loop fusion | flops 75497472 | bytes 69255168 | tf_op jit(solution)/shard_map/reshape.22
  957.9 10.5 convolution_bitcast_fusion
  972.3 11.3 fusion.107
  983.6 17.6 fusion.44
  1001.3 11.8 fusion.106
  1013.2 11.9 fusion.84
  1029.5 10.9 convert_bitcast_fusion.1
  1046.4 7.5 fusion.104
  1061.3 12.2 add_add_fusion
  1073.5 280.0 %all-reduce.17 = bf16[1024,2048]{1,0:T(8,128)(2,1)} all-reduce(f32[1024,2048]{1,0:T(8,128)} %add_add_fusion), channel_id=1, replica_groups=mesh['tp'=4,'cp'=2] {'tp'}, use_global_device_ids=true, to_apply=%region_12.13 | all-reduce | flops 2097152 | bytes 12582912 | tf_op jit(solution)/shard_map/psum | solution.py:125
  1359.4 7.1 fusion.27
  1366.5 60.6 %scatter_custom_fusion = f32[8000,2048]{1,0:T(8,128)} fusion(s32[1024]{0:T(1024)S(1)} %get-tuple-element.11, f32[]{:T(128)} %constant.103.clone.1, f32[1024,2048]{1,0:T(8,128)} %fusion.27, s32[1024]{0:T(1024)S(1)} %broadcast_clamp_fusion), kind=kCustom, calls=%fused_computation.12 | custom fusion | flops 2097152 | bytes 65536512 | tf_op jit(solution)/shard_map/scatter-add | solution.py:128
  1448.5 276.6 %all-reduce.15.cloned.1.call-done = (f32[8000,2048]{1,0:T(8,128)}, f32[2048,512]{1,0:T(8,128)}, f32[2048,512]{1,0:T(8,128)}, f32[2048,512]{1,0:T(8,128)}, f32[51...) async-done(((f32[8000,2048]{1,0:T(8,128)}, f32[2048,512]{1,0:T(8,128)}, f32[2048,512]{1,0:T(8,128)}, f32[2048,512]{1,0:T(8,128)}, ...) | async-done | bytes 116129808 | tf_op jit(solution)/shard_map/psum | solution.py:129
  1725.1 43.1 %copy.101 = f32[8000,2048]{1,0:T(8,128)} copy(f32[8000,2048]{1,0:T(8,128)} %get-tuple-element.62) | data formatting | bytes 131072000
  1782.4 10.4 copy.106
  1792.8 10.4 copy.107
  1803.2 10.5 copy.108
  (173 shorter events, 150.9 us)
Async XLA Ops:
  7.2 250.9 %copy-start = (bf16[512,2048]{1,0:T(8,128)(2,1)S(1)}, bf16[512,2048]{1,0:T(8,128)(2,1)}, u32[]{:S(2)}) copy-start(bf16[512,2048]{1,0:T(8,128)(2,1)} %param.23) | copy-start | bytes 6291460
  7.2 152.5 %all-reduce.9.cloned.1.call-start = ((), (), s32[]{:S(2)}) async-start(), calls=%async_computation.2 | async-start | bytes 8388608 | tf_op jit(solution)/shard_map/psum | solution.py:58
  8.1 35.2 %copy-start.31 = (pred[1024]{0:T(1024)(128)(4,1)}, pred[1024]{0:T(1024)(128)(4,1)S(1)}, u32[]{:S(2)}) copy-start(pred[1024]{0:T(1024)(128)(4,1)S(1)} %get-tuple-element.54) | copy-start | bytes 3076
  47.4 161.1 %all-gather.5.cloned.1.call-start = ((), (), s32[]{:S(2)}) async-start(), calls=%async_computation.4 | async-start | bytes 3145728 | tf_op jit(solution)/shard_map/all_gather | solution.py:71
  47.5 154.5 %copy-start.23 = (f32[2048]{0:T(1024)}, f32[2048]{0:T(1024)S(1)}, u32[]{:S(2)}) copy-start(f32[2048]{0:T(1024)S(1)} %convert_element_type.126) | copy-start | bytes 24580
  50.5 138.7 %copy-start.12 = (f32[1024,64]{1,0:T(8,128)}, f32[1024,64]{1,0:T(8,128)S(1)}, u32[]{:S(2)}) copy-start(f32[1024,64]{1,0:T(8,128)S(1)} %get-tuple-element.53) | copy-start | bytes 786436
  162.8 39.3 %copy-start.27 = (f32[1024]{0:T(1024)}, f32[1024]{0:T(1024)S(1)}, u32[]{:S(2)}) copy-start(f32[1024]{0:T(1024)S(1)} %add_rsqrt_fusion.1) | copy-start | bytes 12292
  196.7 43.5 %all-gather.3.cloned.1.call-start = ((), (), s32[]{:S(2)}) async-start(), calls=%async_computation.3 | async-start | bytes 3145728 | tf_op jit(solution)/shard_map/all_gather | solution.py:72
  208.5 217.1 %all-reduce.11.cloned.1.call-start = ((), (), s32[]{:S(2)}) async-start(), calls=%async_computation.5 | async-start | bytes 16777216 | tf_op jit(solution)/shard_map/psum | solution.py:83
  208.6 17.2 copy-start.7
  265.1 627.8 %all-reduce.13.cloned.1.call-start = ((), (), s32[]{:S(2)}) async-start(), calls=%async_computation.6 | async-start | bytes 16777216 | tf_op jit(solution)/shard_map/psum | solution.py:90
  434.8 11.4 copy-start.14
  434.8 11.4 copy-start.42
  434.8 26.4 %slice-start.2 = ((s8[5636096]{0:T(1024)(128)(4,1)}), s8[1441792]{0:T(1024)(128)(4,1)S(1)}, s32[]{:S(2)}) async-start(s8[5636096]{0:T(1024)(128)(4,1)} %bitcast.129), calls=%async_computation.12 | async-start | bytes 2883584
  446.2 15.0 slice-start.3
  470.6 569.9 %reduce-scatter.3.cloned.1.call-start = ((), (), s32[]{:S(2)}) async-start(), calls=%async_computation.7 | async-start | bytes 6291456 | tf_op jit(solution)/shard_map/reduce_scatter | solution.py:113
  909.6 22.6 %copy-start.40 = (bf16[1024,512]{0,1:T(8,128)(2,1)}, bf16[1024,512]{0,1:T(8,128)(2,1)S(1)}, u32[]{:S(2)}) copy-start(bf16[1024,512]{0,1:T(8,128)(2,1)S(1)} %fusion.51) | copy-start | bytes 3145732
  932.2 25.8 %copy-start.21 = (bf16[1024,4,64]{2,0,1:T(8,128)(2,1)S(1)}, bf16[1024,4,64]{2,0,1:T(8,128)(2,1)}, u32[]{:S(2)}) copy-start(bf16[1024,4,64]{2,0,1:T(8,128)(2,1)} %get-tuple-element.35) | copy-start | bytes 1572868
  932.2 25.8 %copy-start.22 = (bf16[1024,4,64]{2,0,1:T(8,128)(2,1)S(1)}, bf16[1024,4,64]{2,0,1:T(8,128)(2,1)}, u32[]{:S(2)}) copy-start(bf16[1024,4,64]{2,0,1:T(8,128)(2,1)} %get-tuple-element.36) | copy-start | bytes 1572868
  957.9 10.6 copy-start.26
  968.5 91.1 %reduce-scatter.5.cloned.1.call-start = ((), (), s32[]{:S(2)}) async-start(), calls=%async_computation.8 | async-start | bytes 6291456 | tf_op jit(solution)/shard_map/reduce_scatter | solution.py:114
  972.3 11.3 copy-start.9
  1001.3 723.8 %all-reduce.15.cloned.1.call-start = ((), (), s32[]{:S(2)}) async-start(), calls=%async_computation.9 | async-start | bytes 232259584 | tf_op jit(solution)/shard_map/psum | solution.py:129
  1001.3 11.9 copy-start.15
  1001.3 11.9 copy-start.44
  1001.3 23.8 %slice-start = ((s8[8388608]{0:T(1024)(128)(4,1)}), s8[4194304]{0:T(1024)(128)(4,1)S(1)}, s32[]{:S(2)}) async-start(s8[8388608]{0:T(1024)(128)(4,1)} %bitcast.118), calls=%async_computation.10 | async-start | bytes 8388608
  1013.2 11.9 slice-start.1
  1013.2 11.9 copy-start.39
  1029.5 12.8 copy-start.13
  1029.5 12.8 copy-start.19
  1073.5 280.0 %copy-start.24 = (f32[2048]{0:T(1024)S(1)}, f32[2048]{0:T(1024)}, u32[]{:S(2)}) copy-start(f32[2048]{0:T(1024)} %copy-done.23) | copy-start | bytes 24580
  1073.5 280.0 %copy-start.28 = (f32[1024]{0:T(1024)S(1)}, f32[1024]{0:T(1024)}, u32[]{:S(2)}) copy-start(f32[1024]{0:T(1024)} %copy-done.27) | copy-start | bytes 12292
  (25 other events, 118.5 us)
Sparse Core Ops, SparseCore 0:
  47.5 112.0 all-reduce.8
  196.8 7.8 all-gather.4
  208.6 7.8 all-gather.2
  265.2 160.3 all-reduce.10
  470.7 273.2 all-reduce.12
  968.6 8.8 reduce-scatter.2
  1001.4 8.7 reduce-scatter.4
  1443.7 281.3 all-reduce.14
where the time goes:
time: 1830 us; the launch traced here: 1820 us
  blocking collectives  679 us (37%)
  waiting for transfers between devices  536 us (29%)
  matrix products  271 us (15%)
  other arithmetic  170 us (9%)
  local copies, waits for them, and re-layouts  150 us (8%)
    psum x1, blocking collectives, device_step(): d_act_b = to_bf16(lax.psum(d_act_b, 'tp'))  393 us
    psum x1, blocking collectives, device_step(): d_act_a = to_bf16(lax.psum(d_act_a, 'tp'))  280 us
    psum x1, waiting for transfers between devices, device_step(): grad_table = lax.psum(table_part, 'cp')  277 us
    psum x1, waiting for transfers between devices, device_step(): lax.psum(jnp.dot(attended, w_o, preferred_element_type=jnp.float32), 'tp')  150 us
    unnamed x110, local copies, waits for them, and re-layouts  111 us
    psum x1, waiting for transfers between devices, device_step(): embed = lax.psum(picked, 'tp').astype(jnp.float32)  109 us
    scatter-add x3, other arithmetic, device_step(): jax.ops.segment_sum(jnp.where(owned[:, None], d_embed, 0.0), safe_ids, nu...  64.3 us
  transfers between devices with their start and end apart: 8, of which 3 were waited for; matrix products, arithmetic and copies ran while one was open for 10% of the time, Pallas kernels for 0%

commit v1 on v0

v1 whole, which is shorter than its diff:
```python
import functools

import jax
import jax.numpy as jnp
from jax import lax
from jax.experimental import pallas as pl
from jax.experimental.pallas import tpu as pltpu
from jax.sharding import PartitionSpec as P

NORM_EPS = 1e-5
NEG_BIG = -1e30
MESH = pl.DeviceIdType.MESH
NN = (((1,), (0,)), ((), ()))
NT = (((1,), (1,)), ((), ()))
VMEM_LIMIT = 60 * 1024 * 1024
F32 = jnp.float32
BF16 = jnp.bfloat16


def rms_stats(feats):
    inv_rms = lax.rsqrt(jnp.mean(feats * feats, axis=-1, keepdims=True) + NORM_EPS)
    return feats * inv_rms, inv_rms


def rms_back(d_normed, normed, inv_rms):
    return inv_rms * (d_normed - normed * jnp.mean(d_normed * normed, axis=-1, keepdims=True))


def rotate(tensor_in, cosine, sine):
    half = tensor_in.shape[-1] // 2
    first = tensor_in[..., :half]
    second = tensor_in[..., half:]
    return jnp.concatenate([first * cosine - second * sine, second * cosine + first * sine], axis=-1)


def to_bf16(feats):
    return feats.astype(BF16).astype(F32)


def slot_sequence(slot, block_len, cp_count):
    shard = slot // (2 * block_len)
    within = slot % (2 * block_len)
    block_no = jnp.where(within < block_len, shard, 2 * cp_count - 1 - shard)
    return block_no * block_len + within % block_len


def neighbours():
    me = lax.axis_index("tp")
    return me, me + 1 - 2 * lax.rem(me, 2), lax.rem(me + 2, 4), 3 - me


def enter(peers):
    barrier = pltpu.get_barrier_semaphore()
    for peer in peers:
        pl.semaphore_signal(barrier, inc=1, device_id={"tp": peer}, device_id_type=MESH)
    pl.semaphore_wait(barrier, len(peers))


def remote(src, dst, sems, slot, peer):
    return pltpu.make_async_remote_copy(
        src_ref=src, dst_ref=dst, send_sem=sems.at[0, slot], recv_sem=sems.at[1, slot],
        device_id={"tp": peer}, device_id_type=MESH)


def sum_kernel(dims, count, has_add, *refs):
    lhs = refs[:count]
    rhs = refs[count:2 * count]
    rest = refs[2 * count:]
    out_ref, part, recv1, recv2, sems = rest
    wide = part.dtype
    block, half = part.shape[2], part.shape[3]
    me, x_peer, y_peer, diag = neighbours()
    peers = (x_peer, y_peer)
    enter(peers)

    def compute(side, owner):
        rows = pl.ds(pl.multiple_of(owner * block, block), block)
        if dims is None:
            part[side, owner] = lhs[0][rows, side * half:(side + 1) * half]
            return
        tile = 256

        def step(j, carry):
            total = None
            for left, right in zip(lhs, rhs):
                start = pl.multiple_of(side * half + j * tile, tile)
                piece = right[pl.ds(start, tile), :] if dims == NT else right[:, pl.ds(start, tile)]
                term = lax.dot_general(left[rows, :], piece, dims, preferred_element_type=F32)
                total = term if total is None else total + term
            part[side, owner, :, pl.ds(pl.multiple_of(j * tile, tile), tile)] = total
            return carry

        lax.fori_loop(0, half // tile, step, 0)

    first = []
    for k in range(2):
        for side in range(2):
            owner = diag if k == 0 else peers[side]
            compute(side, owner)
            copy = remote(part.at[side, owner], recv1.at[side, k], sems, side * 2 + k, peers[side])
            copy.start()
            first.append(copy)
    for side in range(2):
        compute(side, peers[1 - side])
    for side in range(2):
        compute(side, me)
    second = []
    for side in range(2):
        first[side].wait_recv()
        owner = peers[1 - side]
        part[side, owner] = (part[side, owner].astype(F32) + recv1[side, 0].astype(F32)).astype(wide)
        copy = remote(part.at[side, owner], recv2.at[side], sems, 4 + side, peers[1 - side])
        copy.start()
        second.append(copy)
    mine = pl.ds(pl.multiple_of(me * block, block), block)
    own = []
    for side in range(2):
        first[2 + side].wait_recv()
        second[side].wait_recv()
        total = part[side, me].astype(F32) + recv1[side, 1].astype(F32) + recv2[side].astype(F32)
        cols = slice(side * half, (side + 1) * half)
        out_ref[mine, cols] = total.astype(out_ref.dtype)
        copy = remote(out_ref.at[mine, cols], out_ref.at[mine, cols], sems, 6 + side, peers[1 - side])
        copy.start()
        own.append(copy)
    far = []
    for side in range(2):
        cols = slice(side * half, (side + 1) * half)
        copy = remote(out_ref.at[mine, cols], out_ref.at[mine, cols], sems, 8 + side, peers[side])
        copy.start()
        far.append(copy)
    for side in range(2):
        cols = slice(side * half, (side + 1) * half)
        own[side].wait_recv()
        rows = pl.ds(pl.multiple_of(peers[1 - side] * block, block), block)
        copy = remote(out_ref.at[rows, cols], out_ref.at[rows, cols], sems, 10 + side, peers[side])
        copy.start()
        far.append(copy)
    for copy in far:
        copy.wait_recv()
    for copy in first + second + own + far:
        copy.wait_send()


def tp_sum(lhs, rhs, dims, collective_id):
    span = lhs[0].shape[0]
    width = lhs[0].shape[1] if dims is None else rhs[0].shape[0 if dims == NT else 1]
    block, half = span // 4, width // 2
    wide = BF16 if dims is None else F32
    count = len(lhs)
    vmem = pl.BlockSpec(memory_space=pltpu.VMEM)
    return pl.pallas_call(
        functools.partial(sum_kernel, dims, count, False) if rhs else functools.partial(copy_sum_kernel),
        out_shape=jax.ShapeDtypeStruct((span, width), BF16),
        in_specs=[vmem] * (count + len(rhs)),
        out_specs=vmem,
        scratch_shapes=[
            pltpu.VMEM((2, 4, block, half), wide),
            pltpu.VMEM((2, 2, block, half), wide),
            pltpu.VMEM((2, block, half), wide),
            pltpu.SemaphoreType.DMA((2, 12)),
        ],
        compiler_params=pltpu.CompilerParams(
            collective_id=collective_id, has_side_effects=True, vmem_limit_bytes=VMEM_LIMIT),
        name=f"tp_sum_{collective_id}",
    )(*lhs, *rhs)


def copy_sum_kernel(*refs):
    sum_kernel(None, 1, False, refs[0], None, *refs[1:])


def out_proj_kernel(att_ref, w_ref, embed_ref, res_ref, slots, sems):
    me, x_peer, y_peer, diag = neighbours()
    peers = (x_peer, y_peer)
    enter(peers)
    width = att_ref.shape[1]
    half = att_ref.shape[0] // 2
    sides = [pl.ds(0, half), pl.ds(half, half)]

    def multiply(block, owner, initial):
        tile = 256

        def step(j, carry):
            cols = pl.ds(pl.multiple_of(j * tile, tile), tile)
            rows = pl.ds(pl.multiple_of(owner * width, width), width)
            term = jnp.dot(block[...], w_ref[rows, cols], preferred_element_type=F32)
            if initial:
                res_ref[:, cols] = term
            else:
                res_ref[:, cols] = res_ref[:, cols] + term
            return carry

        lax.fori_loop(0, w_ref.shape[1] // tile, step, 0)

    near = []
    for side in range(2):
        copy = remote(att_ref.at[sides[side]], slots.at[me, sides[side]], sems, side, peers[side])
        copy.start()
        near.append(copy)
    far = []
    for side in range(2):
        copy = remote(att_ref.at[sides[side]], slots.at[me, sides[side]], sems, 2 + side, peers[1 - side])
        copy.start()
        far.append(copy)
    multiply(att_ref, me, True)
    last = []
    for side in range(2):
        near[side].wait_recv()
        owner = peers[side]
        copy = remote(slots.at[owner, sides[side]], slots.at[owner, sides[side]], sems, 4 + side, peers[1 - side])
        copy.start()
        last.append(copy)
    for side in range(2):
        far[side].wait_recv()
    for side in range(2):
        multiply(slots.at[peers[side]], peers[side], False)
    for side in range(2):
        last[side].wait_recv()
    multiply(slots.at[diag], diag, False)
    tile = 256

    def add(j, carry):
        cols = pl.ds(pl.multiple_of(j * tile, tile), tile)
        res_ref[:, cols] = embed_ref[:, cols].astype(F32) + res_ref[:, cols]
        return carry

    lax.fori_loop(0, w_ref.shape[1] // tile, add, 0)
    for copy in near + far + last:
        copy.wait_send()


def out_proj(attended, w_all, embed, collective_id):
    span, width = attended.shape
    vmem = pl.BlockSpec(memory_space=pltpu.VMEM)
    return pl.pallas_call(
        out_proj_kernel,
        out_shape=jax.ShapeDtypeStruct(embed.shape, F32),
        in_specs=[vmem] * 3,
        out_specs=vmem,
        scratch_shapes=[pltpu.VMEM((4, span, width), BF16), pltpu.SemaphoreType.DMA((2, 6))],
        compiler_params=pltpu.CompilerParams(
            collective_id=collective_id, has_side_effects=True, vmem_limit_bytes=VMEM_LIMIT),
        name="out_proj",
    )(attended, w_all, embed)


def solution(mesh):
    cp_count = mesh.shape["cp"]

    def device_step(tokens, pos, doc_id, dy, table, w_q, w_k, w_v, w_o, w_gate, w_up, w_down, gain_one, gain_two, inv_freq):
        span = tokens.shape[0]
        total = span * cp_count
        rows = table.shape[0]
        head_dim = 2 * inv_freq.shape[0]
        kv_local = w_k.shape[1] // head_dim
        q_local = w_q.shape[1] // head_dim
        group = q_local // kv_local
        scale = head_dim ** -0.5
        tp_rank = lax.axis_index("tp")
        cp_rank = lax.axis_index("cp")
        gain_a = gain_one.astype(F32)
        gain_b = gain_two.astype(F32)
        swap = [(0, 1), (1, 0)]

        local_ids = tokens - tp_rank * rows
        owned = (local_ids >= 0) & (local_ids < rows)
        safe_ids = jnp.where(owned, local_ids, 0)
        picked = jnp.where(owned[:, None], jnp.take(table, safe_ids, axis=0), jnp.zeros((), BF16))
        embed_b = tp_sum([picked], [], None, 0)
        embed = embed_b.astype(F32)

        normed_a, inv_a = rms_stats(embed)
        act_a = (normed_a * gain_a).astype(BF16)
        angle = pos.astype(F32)[:, None, None] * inv_freq
        cosine = jnp.cos(angle)
        sine = jnp.sin(angle)
        query = jnp.dot(act_a, w_q, preferred_element_type=F32).reshape(span, q_local, head_dim)
        query = rotate(query, cosine, sine).astype(BF16).reshape(span, kv_local, group, head_dim)
        key_loc = jnp.dot(act_a, w_k, preferred_element_type=F32).reshape(span, kv_local, head_dim)
        key_loc = rotate(key_loc, cosine, sine).astype(BF16)
        value_loc = jnp.dot(act_a, w_v, preferred_element_type=F32).astype(BF16).reshape(span, kv_local, head_dim)

        key_all = lax.all_gather(key_loc, "cp", axis=0, tiled=True)
        value_all = lax.all_gather(value_loc, "cp", axis=0, tiled=True)
        w_tied, key_all, value_all = lax.optimization_barrier((w_o, key_all, value_all))
        w_o_all = lax.all_gather(w_tied, "tp", axis=0, tiled=True)
        doc_all = lax.all_gather(doc_id, "cp", axis=0, tiled=True)
        q_seq = slot_sequence(cp_rank * span + jnp.arange(span), span // 2, cp_count)
        k_seq = slot_sequence(jnp.arange(total), span // 2, cp_count)
        allowed = (doc_id[:, None] == doc_all[None, :]) & (k_seq[None, :] <= q_seq[:, None])

        scores = jnp.einsum("qkgd,skd->kgqs", query, key_all, preferred_element_type=F32) * scale
        attn_prob = jax.nn.softmax(jnp.where(allowed, scores, NEG_BIG), axis=-1)
        prob_b = attn_prob.astype(BF16)
        attended = jnp.einsum("kgqs,skd->qkgd", prob_b, value_all, preferred_element_type=F32)
        attended = attended.astype(BF16).reshape(span, q_local * head_dim)
        residual = out_proj(attended, w_o_all, embed_b, 1)
        normed_b, inv_b = rms_stats(residual)
        act_b = (normed_b * gain_b).astype(BF16)
        gate = jnp.dot(act_b, w_gate, preferred_element_type=F32)
        up_val = jnp.dot(act_b, w_up, preferred_element_type=F32)
        gate_sig = jax.nn.sigmoid(gate)
        hidden = (gate * gate_sig * up_val).astype(BF16)
        d_hidden = to_bf16(jnp.einsum("td,fd->tf", dy, w_down, preferred_element_type=F32))
        d_gate = (d_hidden * up_val * gate_sig * (1.0 + gate * (1.0 - gate_sig))).astype(BF16)
        d_up = (d_hidden * gate * gate_sig).astype(BF16)
        d_act_b = tp_sum([d_gate, d_up], [w_gate, w_up], NT, 2)

        hidden_late, d_act_b = lax.optimization_barrier((hidden, d_act_b))
        out_part = jnp.dot(hidden_late, w_down, preferred_element_type=F32)
        out_mine = lax.psum_scatter(out_part, "tp", scatter_dimension=0, tiled=True)
        res_mine = lax.dynamic_slice_in_dim(residual, tp_rank * (span // 4), span // 4, axis=0)
        layer_out = lax.all_gather((out_mine + res_mine).astype(BF16), "tp", axis=0, tiled=True)

        grad_down = jnp.einsum("tf,td->fd", hidden_late, dy, preferred_element_type=F32)
        grad_gate = jnp.einsum("td,tf->df", act_b, d_gate, preferred_element_type=F32)
        grad_up = jnp.einsum("td,tf->df", act_b, d_up, preferred_element_type=F32)
        d_act_b = d_act_b.astype(F32)
        grad_gain_b = jnp.sum(d_act_b * normed_b, axis=0)
        d_resid = dy.astype(F32) + rms_back(d_act_b * gain_b, normed_b, inv_b)
        d_resid_b = d_resid.astype(BF16)
        grad_out = jnp.einsum("tc,td->cd", attended, d_resid_b, preferred_element_type=F32)
        d_att = jnp.einsum("td,cd->tc", d_resid_b, w_o, preferred_element_type=F32)
        d_att = d_att.astype(BF16).reshape(span, kv_local, group, head_dim)
        d_prob = to_bf16(jnp.einsum("qkgd,skd->kgqs", d_att, value_all, preferred_element_type=F32))
        d_scores = attn_prob * (d_prob - jnp.sum(attn_prob * d_prob, axis=-1, keepdims=True))
        d_scores = (d_scores * scale).astype(BF16)
        d_query = jnp.einsum("kgqs,skd->qkgd", d_scores, key_all, preferred_element_type=F32)
        d_key_all = jnp.einsum("kgqs,qkgd->skd", d_scores, query, preferred_element_type=F32)
        d_value_all = jnp.einsum("kgqs,qkgd->skd", prob_b, d_att, preferred_element_type=F32)
        d_key = lax.psum_scatter(d_key_all, "cp", scatter_dimension=0, tiled=True)
        d_value = lax.psum_scatter(d_value_all, "cp", scatter_dimension=0, tiled=True)
        d_q_pre = rotate(to_bf16(d_query).reshape(span, q_local, head_dim), cosine, -sine)
        d_q_pre = d_q_pre.astype(BF16).reshape(span, q_local * head_dim)
        d_k_pre = rotate(to_bf16(d_key), cosine, -sine).astype(BF16).reshape(span, kv_local * head_dim)
        d_v_pre = d_value.astype(BF16).reshape(span, kv_local * head_dim)
        mlp_grads = lax.psum((grad_gate, grad_up, grad_down), "cp")
        d_act_a = tp_sum([d_q_pre, d_k_pre, d_v_pre], [w_q, w_k, w_v], NT, 3)
        grad_q = jnp.einsum("td,tc->dc", act_a, d_q_pre, preferred_element_type=F32)
        grad_k = jnp.einsum("td,tc->dc", act_a, d_k_pre, preferred_element_type=F32)
        grad_v = jnp.einsum("td,tc->dc", act_a, d_v_pre, preferred_element_type=F32)
        d_act_a = d_act_a.astype(F32)
        grad_gain_a = jnp.sum(d_act_a * normed_a, axis=0)
        d_embed = d_resid + rms_back(d_act_a * gain_a, normed_a, inv_a)
        d_embed_other = lax.ppermute(d_embed, "cp", swap)
        tokens_other = lax.ppermute(tokens, "cp", swap)
        even = cp_rank == 0
        all_ids = jnp.where(even, jnp.concatenate([tokens, tokens_other]), jnp.concatenate([tokens_other, tokens])) - tp_rank * rows
        all_grads = jnp.where(even, jnp.concatenate([d_embed, d_embed_other]), jnp.concatenate([d_embed_other, d_embed]))
        all_ids = jnp.where((all_ids >= 0) & (all_ids < rows), all_ids, rows)
        grad_table = jax.ops.segment_sum(all_grads, all_ids, num_segments=rows)
        att_grads = lax.psum((grad_q, grad_k, grad_v, grad_out), "cp")
        gains = lax.psum((grad_gain_a, grad_gain_b), "cp")
        grad_gate, grad_up, grad_down = mlp_grads
        return (layer_out, grad_table) + tuple(att_grads) + (grad_gate, grad_up, grad_down) + tuple(gains)

    col_spec = P(None, "tp")
    row_spec = P("tp", None)
    tok_spec = P("cp")
    rep_spec = P(None)
    in_specs = (tok_spec, tok_spec, tok_spec, P("cp", None), row_spec, col_spec, col_spec, col_spec, row_spec, col_spec, col_spec, row_spec, rep_spec, rep_spec, rep_spec)
    out_specs = (P("cp", None), row_spec, col_spec, col_spec, col_spec, row_spec, col_spec, col_spec, row_spec, rep_spec, rep_spec)
    return jax.shard_map(device_step, mesh=mesh, in_specs=in_specs, out_specs=out_specs, check_vma=False)
```

time: 1830 us -> 962 us (0.53)
  blocking collectives: 679 us -> 6.22 us
  waiting for transfers between devices: 536 us -> 26.3 us
  Pallas kernels: 0 us -> 368 us
  matrix products: 271 us -> 210 us
  other arithmetic: 170 us -> 208 us
  local copies, waits for them, and re-layouts: 150 us -> 119 us
    psum x3 -> x1, blocking collectives: 677 us -> 3.9 us  [device_step(): gains = lax.psum((grad_gain_a, grad_gain_b), 'cp')]
    psum x4 -> x1, waiting for transfers between devices: 535 us -> 0.01 us  [device_step(): att_grads = lax.psum((grad_q, grad_k, grad_v, grad_out), 'cp')]
    pallas_call x0 -> x4, Pallas kernels: none -> 368 us  [the longest x3 319 us: tp_sum(): pl.pallas_call(functools.partial(sum_kernel, dims, count, False) if rhs e...]
    dot_general x27 -> x21, matrix products: 271 us -> 210 us  [the longest x1 23.6 us: device_step(): jnp.einsum('qkgd,skd->kgqs', d_att, value_all, preferred_element_type=F32)]
    unnamed x110 -> x102, local copies, waits for them, and re-layouts: 111 us -> 74.6 us
    scatter-add x3, other arithmetic: 64.3 us -> 89.4 us  [device_step(): grad_table = jax.ops.segment_sum(all_grads, all_ids, num_segments=rows)]
  transfers between devices with their start and end apart: 8 -> 10, of which waited for: 3 -> 3; matrix products, arithmetic and copies ran while one was open for 10% -> 42% of each run, Pallas kernels for 0% -> 12%
where the time goes in v1:
time: 962 us; the launch traced here: 954 us
  Pallas kernels  368 us (38%)
  matrix products  210 us (22%)
  other arithmetic  208 us (22%)
  local copies, waits for them, and re-layouts  119 us (12%)
  waiting for transfers between devices  26.3 us (3%)
  between operations  15 us (2%)
    pallas_call x3, Pallas kernels, tp_sum(): pl.pallas_call(functools.partial(sum_kernel, dims, count, False) if rhs e...  319 us
    scatter-add x3, other arithmetic, device_step(): grad_table = jax.ops.segment_sum(all_grads, all_ids, num_segments=rows)  89.4 us
    unnamed x102, local copies, waits for them, and re-layouts  74.6 us
    pallas_call x1, Pallas kernels, out_proj(): pl.pallas_call(out_proj_kernel, out_shape=jax.ShapeDtypeStruct(embed.shap...  48.9 us
    gather x1, local copies, waits for them, and re-layouts, device_step(): jnp.take(table, safe_ids, axis=0)  35.9 us
    another operation x3, other arithmetic  32.4 us
    dot_general x1, matrix products, device_step(): jnp.einsum('qkgd,skd->kgqs', d_att, value_all, preferred_element_type=F32)  23.6 us
  transfers between devices with their start and end apart: 10, of which 3 were waited for; matrix products, arithmetic and copies ran while one was open for 42% of the time, Pallas kernels for 12%

profile of v1, /device:TPU:0, one launch (start us, length us, event | category | flops | bytes accessed | tf_op | source)
XLA Modules:
  0.0 953.8 jit_solution(641943155440408257)
XLA Ops:
  9.3 35.9 %gather_fusion = bf16[1024,2048]{1,0:T(8,128)(2,1)} fusion(bf16[8000,2048]{1,0:T(8,128)(2,1)} %param.19, s32[1024]{0:T(1024)S(1)} %fusion.78), kind=kCustom, calls=%fused_computation | custom fusion | bytes 8392704 | tf_op jit(solution)/shard_map/jit(_take)/gather | solution.py:269
  49.3 93.0 %tp_sum_0.1.embed_ref = bf16[1024,2048]{1,0:T(8,128)(2,1)} custom-call(bf16[1024,2048]{1,0:T(8,128)(2,1)} %select_select_fusion.refs_0_), custom_call_target="tpu_custom_call" | custom-call | tf_op jit(solution)/shard_map/tp_sum_0/pallas_call | solution.py:152
  151.8 5.4 fusion.89
  183.4 8.9 all-gather.5.cloned.1.call-done
  192.4 8.3 copy.97.refs_2_
  200.7 8.3 copy.98.refs_3_
  213.8 11.4 %convolution_convert_fusion.1 = bf16[1024,1376]{1,0:T(8,128)(2,1)} fusion(bf16[1024,2048]{1,0:T(8,128)(2,1)} %param.18, bf16[1376,2048]{1,0:T(8,128)(2,1)} %param.26), kind=kOutput, calls=%fused_computation.61 | convolution fusion | flops 5772771328 | bytes 12648448 | tf_op jit(solution)/shard_map/td,fd->tf/dot_general | solution.py:305
  225.2 15.0 %fusion.11 = (f32[4,1024]{1,0:T(4,128)S(1)}, f32[4,2048,1024]{2,1,0:T(8,128)}) fusion(pred[1024,2048]{0,1:T(8,128)(4,1)S(1)} %compare_and_fusion, bf16[2048,4,128]{2,0,1:T(8,128)(2,1)S(1)} %copy-done.6, bf16[1024,4,64]{2,0,1:T(8,128)(2,1)S(1)} %copy-done.26, bf16[1024,4,64]{2,0,1:T(8,128)(2,1)S(1)} %get-tuple-element.39), kind=kOutput, calls=%fused_computation.16 | convolution fusion | flops 2174742528 | bytes 38813696 | tf_op jit(solution)/shard_map/qkgd,skd->kgqs/dot_general | solution.py:293
  240.2 14.4 %fusion.10 = f32[4,1024]{1,0:T(4,128)S(1)} fusion(f32[4,2048,1024]{2,1,0:T(8,128)} %get-tuple-element.61, f32[4,1024]{1,0:T(4,128)S(1)} %get-tuple-element.60, pred[1024,2048]{0,1:T(8,128)(4,1)S(1)} %compare_and_fusion), kind=kLoop, calls=%fused_computation.15 | loop fusion | flops 33550336 | bytes 35684352 | tf_op jit(solution)/shard_map/reduce_sum | solution.py:294
  254.6 16.6 %fusion.52 = bf16[4,128,1024]{2,1,0:T(8,128)(2,1)S(1)} fusion(bf16[2048,4,128]{2,0,1:T(8,128)(2,1)} %all-gather.7.cloned.1.call-done, f32[4,1024]{1,0:T(4,128)S(1)} %fusion.10, f32[4,1024]{1,0:T(4,128)S(1)} %get-tuple-element.60, f32[4,2048,1024]{2,1,0:T(8,128)} %get-tuple-element.61, pred[1024,2048]{0,1:T(8,128)(4,1)S(1)} %compare_and_fusion), kind=kOutput, calls=%fused_computation.80 | convolution fusion | flops 2189950976 | bytes 38830080 | tf_op jit(solution)/shard_map/kgqs,skd->qkgd/dot_general | solution.py:296
  277.1 48.9 %out_proj.1 = f32[1024,2048]{1,0:T(8,128)} custom-call(bf16[1024,512]{1,0:T(8,128)(2,1)} %copy.123.att_ref, bf16[2048,2048]{1,0:T(8,128)(2,1)} %all-gather.9.cloned.1.call-done.w_ref, bf16[1024,2048]{1,0:T(8,128)(2,1)} %tp_sum_0.1.embed_ref), custom_call_target="tpu_custom_call" | custom-call | tf_op jit(solution)/shard_map/out_proj/pallas_call | solution.py:236
  333.6 8.5 fusion.96
  342.1 15.0 %fusion.39 = (bf16[1024,1376]{1,0:T(8,128)(2,1)}, bf16[1024,1376]{1,0:T(8,128)(2,1)}, bf16[1024,1376]{1,0:T(8,128)(2,1)}) fusion(bf16[1024,1376]{1,0:T(8,128)(2,1)} %convolution_convert_fusion.1, f32[1024,1376]{1,0:T(8,128)} %fusion.96, bf16[1024,2048]{1,0:T(8,128)(2,1)S(1)} %multiply_convert_fusion, bf16[2048,1376]{0,1:T(8,128)(2,1)} %param.25), kind=kOutput, calls=%fused_computation.55 | convolution fusion | flops 5795315712 | bytes 26738688 | tf_op jit(solution)/shard_map/dot_general | solution.py:302
  357.2 115.7 %tp_sum_2.1 = bf16[1024,2048]{1,0:T(8,128)(2,1)} custom-call(bf16[1024,1376]{1,0:T(8,128)(2,1)} %get-tuple-element.36.refs_0_, bf16[1024,1376]{1,0:T(8,128)(2,1)} %get-tuple-element.38.refs_1_, bf16[2048,1376]{1,0:T(8,128)(2,1)} %copy.97.refs_2_, bf16[2048,1376]{1,0:T(8,128)(2,1)} %copy.98.refs_3_), custom_call_target="tpu_custom_call" | custom-call | tf_op jit(solution)/shard_map/tp_sum_2/pallas_call | solution.py:152
  472.9 11.5 %fusion.97 = f32[1024,2048]{1,0:T(8,128)} fusion(bf16[1024,1376]{1,0:T(8,128)(2,1)} %get-tuple-element.19, bf16[1376,2048]{1,0:T(8,128)(2,1)} %param.26), kind=kOutput, calls=%fused_computation.154 | convolution fusion | flops 5771362304 | bytes 16842752 | tf_op jit(solution)/shard_map/dot_general | solution.py:311
  484.5 7.1 fusion.35
  499.9 17.7 %fusion.42 = f32[2048,4,128]{0,2,1:T(8,128)} fusion(bf16[1024,4,128]{0,2,1:T(8,128)(2,1)S(1)} %bitcast.135, f32[4,1024]{1,0:T(4,128)S(1)} %fusion.10, f32[4,1024]{1,0:T(4,128)S(1)} %get-tuple-element.60, f32[4,2048,1024]{2,1,0:T(8,128)} %get-tuple-element.61, pred[1024,2048]{0,1:T(8,128)(4,1)S(1)} %compare_and_fusion), kind=kOutput, calls=%fused_computation.62 | convolution fusion | flops 2189426688 | bytes 40927232 | tf_op jit(solution)/shard_map/kgqs,qkgd->skd/dot_general | solution.py:331
  517.5 23.6 %fusion.3 = (f32[4,1024]{1,0:T(4,128)S(1)}, bf16[4,2048,1024]{2,1,0:T(8,128)(2,1)}) fusion(f32[4,1024]{1,0:T(4,128)S(1)} %fusion.10, f32[4,1024]{1,0:T(4,128)S(1)} %get-tuple-element.60, f32[4,2048,1024]{2,1,0:T(8,128)} %get-tuple-element.61, pred[1024,2048]{0,1:T(8,128)(4,1)S(1)} %compare_and_fusion, ...), kind=kOutput, calls=%fused_computation.7 | convolution fusion | flops 2214588416 | bytes 55623680 | tf_op jit(solution)/shard_map/qkgd,skd->kgqs/dot_general | solution.py:326
  541.3 25.9 %fusion.12 = bf16[4,1024,2048]{1,2,0:T(8,128)(2,1)} fusion(bf16[4,2048,1024]{2,1,0:T(8,128)(2,1)} %get-tuple-element.63, f32[4,1024]{1,0:T(4,128)S(1)} %get-tuple-element.62, f32[4,1024]{1,0:T(4,128)S(1)} %fusion.10, f32[4,1024]{1,0:T(4,128)S(1)} %get-tuple-element.60, f32[4,2048,1024]{2,1,0:T(8,128)} %get-tuple-element.61, ...), kind=kLoop, calls=%fused_computation.17 | loop fusion | flops 75497472 | bytes 69255168 | tf_op jit(solution)/shard_map/reshape.22
  567.2 10.4 %convolution_bitcast_fusion = f32[2048,4,128]{2,0,1:T(8,128)} fusion(bf16[4,1024,2048]{1,2,0:T(8,128)(2,1)} %fusion.12, bf16[1024,4,64]{2,0,1:T(8,128)(2,1)S(1)} %copy-done.27, bf16[1024,4,64]{2,0,1:T(8,128)(2,1)S(1)} %copy-done.25), kind=kOutput, calls=%fused_computation.63 | convolution fusion | flops 2149580800 | bytes 22020096 | tf_op jit(solution)/shard_map/kgqs,qkgd->skd/dot_general | solution.py:330
  577.7 10.5 %fusion.98 = f32[2048,1376]{0,1:T(8,128)} fusion(bf16[1024,2048]{1,0:T(8,128)(2,1)} %copy-done.9, bf16[1024,1376]{1,0:T(8,128)(2,1)S(1)} %copy-done.18), kind=kOutput, calls=%fused_computation.155 | convolution fusion | flops 5771362304 | bytes 18284544 | tf_op jit(solution)/shard_map/td,tf->df/dot_general | solution.py:317
  588.2 8.9 fusion.99
  601.0 7.7 fusion.45
  608.7 9.9 %convert_bitcast_fusion.1 = f32[1024,4,128]{2,0,1:T(8,128)S(1)} fusion(bf16[2048,4,128]{2,0,1:T(8,128)(2,1)} %all-gather.5.cloned.1.call-done, bf16[4,1024,2048]{1,2,0:T(8,128)(2,1)} %fusion.12), kind=kOutput, calls=%fused_computation.64 | convolution fusion | flops 2148532224 | bytes 20971520 | tf_op jit(solution)/shard_map/kgqs,skd->qkgd/dot_general | solution.py:329
  618.6 11.6 %fusion.100 = f32[1376,2048]{1,0:T(8,128)} fusion(bf16[1024,1376]{1,0:T(8,128)(2,1)} %get-tuple-element.19, bf16[1024,2048]{1,0:T(8,128)(2,1)} %param.18), kind=kOutput, calls=%fused_computation.157 | convolution fusion | flops 5771362304 | bytes 18284544 | tf_op jit(solution)/shard_map/tf,td->fd/dot_general | solution.py:316
  656.3 110.0 %tp_sum_3.1 = bf16[1024,2048]{1,0:T(8,128)(2,1)} custom-call(bf16[1024,512]{1,0:T(8,128)(2,1)} %bitcast.125, bf16[1024,512]{1,0:T(8,128)(2,1)} %bitcast.126, bf16[1024,512]{1,0:T(8,128)(2,1)} %copy.124.refs_2_, bf16[2048,512]{1,0:T(8,128)(2,1)} %refs_3_.2, bf16[2048,512]{1,0:T(8,128)(2,1)} %refs_4_.1, bf16[2048,512]{1,0:T(8,128)(2,1)} %refs_5_.1), custom_call_target="tpu_custom_call" | custom-call | tf_op jit(solution)/shard_map/tp_sum_3/pallas_call | solution.py:152
  772.3 6.8 fusion.28
  779.7 12.7 %collective-permute-done = s32[1024]{0:T(1024)S(1)} collective-permute-done((s32[1024]{0:T(1024)S(1)}, s32[1024]{0:T(1024)S(1)}, u32[]{:S(2)}, u32[]{:S(2)}) %collective-permute-start) | collective-permute-done | bytes 4128 | tf_op jit(solution)/shard_map/ppermute | solution.py:347
  800.7 17.5 %maximum_select_fusion = f32[2048,2048]{1,0:T(8,128)} fusion(f32[1024,2048]{1,0:T(8,128)} %collective-permute-done.1, f32[1024,2048]{1,0:T(8,128)} %fusion.28, pred[]{:T(512)S(6)} %eq.25), kind=kLoop, calls=%fused_computation.19 | loop fusion | flops 12582912 | bytes 33554432 | tf_op jit(solution)/shard_map/jit(_where)/select_n | solution.py:350
  818.2 85.0 %scatter_custom_fusion = f32[8000,2048]{1,0:T(8,128)} fusion(s32[2048]{0:T(1024)S(1)} %get-tuple-element.21, f32[]{:T(128)} %constant.106.clone.1, f32[2048,2048]{1,0:T(8,128)} %maximum_select_fusion, s32[2048]{0:T(1024)S(1)} %broadcast_clamp_fusion), kind=kCustom, calls=%fused_computation.12 | custom fusion | flops 4194304 | bytes 65536512 | tf_op jit(solution)/shard_map/scatter-add | solution.py:352
  921.3 10.5 %copy.150 = f32[2048,1376]{0,1:T(8,128)} copy(f32[2048,1376]{0,1:T(8,128)} %get-tuple-element.83) | data formatting | bytes 22544384
  931.8 10.5 %copy.151 = f32[2048,1376]{0,1:T(8,128)} copy(f32[2048,1376]{0,1:T(8,128)} %get-tuple-element.84) | data formatting | bytes 22544384
  (171 shorter events, 135.5 us)
Async XLA Ops:
  7.2 176.3 %all-gather.7.cloned.1.call-start = ((), (), s32[]{:S(2)}) async-start(), calls=%async_computation.4 | async-start | bytes 3145728 | tf_op jit(solution)/shard_map/all_gather | solution.py:285
  9.3 152.8 %copy-start.28 = (f32[2048]{0:T(1024)}, f32[2048]{0:T(1024)S(1)}, u32[]{:S(2)}) copy-start(f32[2048]{0:T(1024)S(1)} %convert_element_type.120) | copy-start | bytes 24580
  49.3 96.1 %copy-start.20 = (bf16[2048,512]{1,0:T(8,128)(2,1)S(1)}, bf16[2048,512]{1,0:T(8,128)(2,1)}, u32[]{:S(2)}) copy-start(bf16[2048,512]{1,0:T(8,128)(2,1)} %refs_5_.1) | copy-start | bytes 6291460
  145.4 16.7 %copy-start.31 = (f32[1024]{0:T(1024)}, f32[1024]{0:T(1024)S(1)}, u32[]{:S(2)}) copy-start(f32[1024]{0:T(1024)S(1)} %add_rsqrt_fusion.1) | copy-start | bytes 12292
  151.5 40.9 %all-gather.5.cloned.1.call-start = ((), (), s32[]{:S(2)}) async-start(), calls=%async_computation.3 | async-start | bytes 3145728 | tf_op jit(solution)/shard_map/all_gather | solution.py:284
  181.8 43.4 %copy-start.24 = (bf16[1024,4,64]{2,0,1:T(8,128)(2,1)}, bf16[1024,4,64]{2,0,1:T(8,128)(2,1)S(1)}, u32[]{:S(2)}) copy-start(bf16[1024,4,64]{2,0,1:T(8,128)(2,1)S(1)} %get-tuple-element.39) | copy-start | bytes 1572868
  181.8 10.6 %copy-start.35 = (bf16[2048]{0:T(1024)(128)(2,1)S(1)}, bf16[2048]{0:T(1024)(128)(2,1)}, u32[]{:S(2)}) copy-start(bf16[2048]{0:T(1024)(128)(2,1)} %param.28) | copy-start | bytes 12292
  183.4 93.8 %all-gather.9.cloned.1.call-start = ((), (), s32[]{:S(2)}) async-start(), calls=%async_computation.5 | async-start | bytes 10485760 | tf_op jit(solution)/shard_map/all_gather | solution.py:287
  192.4 404.8 %reduce-scatter.4.cloned.1.call-start = ((), (), s32[]{:S(2)}) async-start(), calls=%async_computation.6 | async-start | bytes 10485760 | tf_op jit(solution)/shard_map/reduce_scatter | solution.py:312
  200.7 8.3 copy-start.34
  213.8 11.4 %copy-start.6 = (bf16[2048,4,128]{2,0,1:T(8,128)(2,1)S(1)}, bf16[2048,4,128]{2,0,1:T(8,128)(2,1)}, u32[]{:S(2)}) copy-start(bf16[2048,4,128]{2,0,1:T(8,128)(2,1)} %all-gather.5.cloned.1.call-done) | copy-start | bytes 6291460
  213.8 11.4 %copy-start.26 = (bf16[1024,4,64]{2,0,1:T(8,128)(2,1)S(1)}, bf16[1024,4,64]{2,0,1:T(8,128)(2,1)}, u32[]{:S(2)}) copy-start(bf16[1024,4,64]{2,0,1:T(8,128)(2,1)} %get-tuple-element.40) | copy-start | bytes 1572868
  271.3 54.8 %copy-start.22 = (bf16[4,128,1024]{2,1,0:T(8,128)(2,1)}, bf16[4,128,1024]{2,1,0:T(8,128)(2,1)S(1)}, u32[]{:S(2)}) copy-start(bf16[4,128,1024]{2,1,0:T(8,128)(2,1)S(1)} %fusion.52) | copy-start | bytes 3145732
  333.6 8.5 copy-start.9
  484.5 145.8 %reduce-scatter.8.cloned.1.call-start = ((), (), s32[]{:S(2)}) async-start(), calls=%async_computation.9 | async-start | bytes 6291456 | tf_op jit(solution)/shard_map/reduce_scatter | solution.py:333
  484.5 7.1 copy-start.4
  484.5 7.1 copy-start.16
  499.9 17.7 %copy-start.38 = (bf16[1024,512]{0,1:T(8,128)(2,1)}, bf16[1024,512]{0,1:T(8,128)(2,1)S(1)}, u32[]{:S(2)}) copy-start(bf16[1024,512]{0,1:T(8,128)(2,1)S(1)} %fusion.49) | copy-start | bytes 3145732
  541.2 91.9 %reduce-scatter.6.cloned.1.call-start = ((), (), s32[]{:S(2)}) async-start(), calls=%async_computation.8 | async-start | bytes 6291456 | tf_op jit(solution)/shard_map/reduce_scatter | solution.py:332
  541.2 25.9 %copy-start.25 = (bf16[1024,4,64]{2,0,1:T(8,128)(2,1)S(1)}, bf16[1024,4,64]{2,0,1:T(8,128)(2,1)}, u32[]{:S(2)}) copy-start(bf16[1024,4,64]{2,0,1:T(8,128)(2,1)} %copy-done.24) | copy-start | bytes 1572868
  541.2 25.9 %copy-start.27 = (bf16[1024,4,64]{2,0,1:T(8,128)(2,1)S(1)}, bf16[1024,4,64]{2,0,1:T(8,128)(2,1)}, u32[]{:S(2)}) copy-start(bf16[1024,4,64]{2,0,1:T(8,128)(2,1)} %get-tuple-element.40) | copy-start | bytes 1572868
  567.2 10.5 %copy-start.18 = (bf16[1024,1376]{1,0:T(8,128)(2,1)S(1)}, bf16[1024,1376]{1,0:T(8,128)(2,1)}, u32[]{:S(2)}) copy-start(bf16[1024,1376]{1,0:T(8,128)(2,1)} %get-tuple-element.36.refs_0_) | copy-start | bytes 8454148
  577.6 325.6 %all-gather.11.cloned.1.call-start = ((), (), s32[]{:S(2)}) async-start(), calls=%async_computation.7 | async-start | bytes 5242880 | tf_op jit(solution)/shard_map/all_gather | solution.py:314
  577.7 10.6 %copy-start.10 = (bf16[1024,2048]{1,0:T(8,128)(2,1)S(1)}, bf16[1024,2048]{1,0:T(8,128)(2,1)}, u32[]{:S(2)}) copy-start(bf16[1024,2048]{1,0:T(8,128)(2,1)} %copy-done.9) | copy-start | bytes 12582916
  577.7 10.5 %copy-start.17 = (bf16[1024,1376]{1,0:T(8,128)(2,1)S(1)}, bf16[1024,1376]{1,0:T(8,128)(2,1)}, u32[]{:S(2)}) copy-start(bf16[1024,1376]{1,0:T(8,128)(2,1)} %get-tuple-element.38.refs_1_) | copy-start | bytes 8454148
  600.7 302.4 %all-reduce.4.cloned.1.call-start = ((), (), s32[]{:S(2)}) async-start(), calls=%async_computation.10 | async-start | bytes 101187584 | tf_op jit(solution)/shard_map/psum | solution.py:353
  772.3 24.5 %copy-start.33 = (f32[2048]{0:T(1024)S(1)}, f32[2048]{0:T(1024)}, u32[]{:S(2)}) copy-start(f32[2048]{0:T(1024)} %get-tuple-element.23) | copy-start | bytes 24580
  779.2 21.5 %collective-permute-start.1 = (f32[1024,2048]{1,0:T(8,128)}, f32[1024,2048]{1,0:T(8,128)}, u32[]{:S(2)}, u32[]{:S(2)}) collective-permute-start(f32[1024,2048]{1,0:T(8,128)} %fusion.28), channel_id=1, source_target_pairs={{0,1},{1,0},{2,3},{3,2},{4,5},{5,4},{6,7},{7,6}} | collective-permute-start | bytes 25165832 | tf_op jit(solution)/shard_map/ppermute | solution.py:346
  779.2 13.2 %collective-permute-start = (s32[1024]{0:T(1024)S(1)}, s32[1024]{0:T(1024)S(1)}, u32[]{:S(2)}, u32[]{:S(2)}) collective-permute-start(s32[1024]{0:T(1024)S(1)} %copy-done.30), channel_id=1, source_target_pairs={{0,1},{1,0},{2,3},{3,2},{4,5},{5,4},{6,7},{7,6}} | collective-permute-start | bytes 12296 | tf_op jit(solution)/shard_map/ppermute | solution.py:347
  921.3 21.1 %slice-start = ((s8[11272192]{0:T(1024)(128)(4,1)}), s8[4194304]{0:T(1024)(128)(4,1)S(1)}, s32[]{:S(2)}) async-start(s8[11272192]{0:T(1024)(128)(4,1)} %bitcast.119), calls=%async_computation.11 | async-start | bytes 8388608
  921.3 21.1 %slice-start.1 = ((s8[11272192]{0:T(1024)(128)(4,1)}), s8[4194304]{0:T(1024)(128)(4,1)S(1)}, s32[]{:S(2)}) async-start(s8[11272192]{0:T(1024)(128)(4,1)} %bitcast.119), calls=%async_computation.12 | async-start | bytes 8388608
  931.8 10.6 %slice-start.2 = ((s8[11272192]{0:T(1024)(128)(4,1)}), s8[2883584]{0:T(1024)(128)(4,1)S(1)}, s32[]{:S(2)}) async-start(s8[11272192]{0:T(1024)(128)(4,1)} %bitcast.119), calls=%async_computation.13 | async-start | bytes 5767168
  (22 other events, 97.1 us)
Sparse Core Ops, SparseCore 0:
  151.6 8.7 all-gather.6
  183.5 8.7 all-gather.4
  194.1 82.9 all-gather.8
  484.6 80.5 reduce-scatter.3
  567.8 8.7 reduce-scatter.7
  579.3 9.8 reduce-scatter.5
  600.9 46.6 all-gather.10
  652.8 126.6 all-reduce.3

commit v2 on v1

v2 whole, which is shorter than its diff:
```python
import functools

import jax
import jax.numpy as jnp
from jax import lax
from jax.experimental import pallas as pl
from jax.experimental.pallas import tpu as pltpu
from jax.sharding import PartitionSpec as P

NORM_EPS = 1e-5
NEG_BIG = -1e30
MESH = pl.DeviceIdType.MESH
NN = (((1,), (0,)), ((), ()))
NT = (((1,), (1,)), ((), ()))
VMEM_LIMIT = 60 * 1024 * 1024
F32 = jnp.float32
BF16 = jnp.bfloat16


def rms_stats(feats):
    inv_rms = lax.rsqrt(jnp.mean(feats * feats, axis=-1, keepdims=True) + NORM_EPS)
    return feats * inv_rms, inv_rms


def rms_back(d_normed, normed, inv_rms):
    return inv_rms * (d_normed - normed * jnp.mean(d_normed * normed, axis=-1, keepdims=True))


def to_bf16(feats):
    return feats.astype(BF16).astype(F32)


def neighbours():
    me = lax.axis_index("tp")
    return me, me + 1 - 2 * lax.rem(me, 2), lax.rem(me + 2, 4), 3 - me


def enter(peers):
    barrier = pltpu.get_barrier_semaphore()
    for peer in peers:
        pl.semaphore_signal(barrier, inc=1, device_id={"tp": peer}, device_id_type=MESH)
    pl.semaphore_wait(barrier, len(peers))


def remote(src, dst, sems, slot, peer):
    return pltpu.make_async_remote_copy(
        src_ref=src, dst_ref=dst, send_sem=sems.at[0, slot], recv_sem=sems.at[1, slot],
        device_id={"tp": peer}, device_id_type=MESH)


def tp_exchange(compute, done, out_ref, part, recv1, recv2, sems):
    wide = part.dtype
    block, half = part.shape[2], part.shape[3]
    me, x_peer, y_peer, diag = neighbours()
    peers = (x_peer, y_peer)

    first = []
    for k in range(2):
        for side in range(2):
            owner = diag if k == 0 else peers[side]
            compute(side, owner)
            copy = remote(part.at[side, owner], recv1.at[side, k], sems, side * 2 + k, peers[side])
            copy.start()
            first.append(copy)
    for side in range(2):
        compute(side, peers[1 - side])
    for side in range(2):
        compute(side, me)
    second = []
    for side in range(2):
        first[side].wait_recv()
        owner = peers[1 - side]
        part[side, owner] = (part[side, owner].astype(F32) + recv1[side, 0].astype(F32)).astype(wide)
        copy = remote(part.at[side, owner], recv2.at[side], sems, 4 + side, peers[1 - side])
        copy.start()
        second.append(copy)
    mine = pl.ds(pl.multiple_of(me * block, block), block)
    sides = [slice(side * half, (side + 1) * half) for side in range(2)]
    own = []
    for side in range(2):
        first[2 + side].wait_recv()
        second[side].wait_recv()
        total = part[side, me].astype(F32) + recv1[side, 1].astype(F32) + recv2[side].astype(F32)
        out_ref[mine, sides[side]] = total.astype(out_ref.dtype)
        copy = remote(out_ref.at[mine, sides[side]], out_ref.at[mine, sides[side]], sems, 6 + side, peers[1 - side])
        copy.start()
        own.append(copy)
    far = []
    for side in range(2):
        copy = remote(out_ref.at[mine, sides[side]], out_ref.at[mine, sides[side]], sems, 8 + side, peers[side])
        copy.start()
        far.append(copy)
    done(me)
    for side in range(2):
        own[side].wait_recv()
        rows = pl.ds(pl.multiple_of(peers[1 - side] * block, block), block)
        copy = remote(out_ref.at[rows, sides[side]], out_ref.at[rows, sides[side]], sems, 10 + side, peers[side])
        copy.start()
        far.append(copy)
    for side in range(2):
        far[side].wait_recv()
    done(x_peer)
    done(y_peer)
    for side in range(2):
        far[2 + side].wait_recv()
    done(diag)
    for copy in first + second + own + far:
        copy.wait_send()


def exchange_scratch(span, width, wide):
    block, half = span // 4, width // 2
    return [
        pltpu.VMEM((2, 4, block, half), wide),
        pltpu.VMEM((2, 2, block, half), wide),
        pltpu.VMEM((2, block, half), wide),
        pltpu.SemaphoreType.DMA((2, 12)),
    ]


EXCHANGE_COST = pl.CostEstimate(flops=10**11, bytes_accessed=10**8, transcendentals=0)


def comm_params(collective_id):
    return pltpu.CompilerParams(collective_id=collective_id, has_side_effects=True, vmem_limit_bytes=VMEM_LIMIT)


VMEM_SPEC = pl.BlockSpec(memory_space=pltpu.VMEM)


def product_into(part, lhs, rhs, dims):
    block, half = part.shape[2], part.shape[3]
    tile = 256

    def compute(side, owner):
        rows = pl.ds(pl.multiple_of(owner * block, block), block)

        def step(j, carry):
            total = None
            for left, right in zip(lhs, rhs):
                start = pl.multiple_of(side * half + j * tile, tile)
                piece = right[pl.ds(start, tile), :] if dims == NT else right[:, pl.ds(start, tile)]
                term = lax.dot_general(left[rows, :], piece, dims, preferred_element_type=F32)
                total = term if total is None else total + term
            part[side, owner, :, pl.ds(pl.multiple_of(j * tile, tile), tile)] = total
            return carry

        lax.fori_loop(0, half // tile, step, 0)

    return compute


def inverse_root(value):
    guess = lax.rsqrt(value)
    return guess * (1.5 - 0.5 * value * guess * guess)


def turn(feats, cosine, sine):
    return feats * cosine + pltpu.roll(feats, feats.shape[-1] // 2, 1) * sine


def embed_kernel(picked, gain, w_q, w_k, w_v, cosine, sine, embed, act, q_ref, k_ref, v_ref, part, recv1, recv2, sems, kv_sems):
    block, half = part.shape[2], part.shape[3]
    span = picked.shape[0]
    head = cosine.shape[1]
    me, x_peer, y_peer, diag = neighbours()
    cp = lax.axis_index("cp")
    barrier = pltpu.get_barrier_semaphore()
    for peer in ({"tp": x_peer}, {"tp": y_peer}, {"cp": 1 - cp}):
        pl.semaphore_signal(barrier, inc=1, device_id=peer, device_id_type=MESH)
    pl.semaphore_wait(barrier, 3)
    sent = []

    def compute(side, owner):
        rows = pl.ds(pl.multiple_of(owner * block, block), block)
        part[side, owner] = picked[rows, side * half:(side + 1) * half]

    def done(owner):
        rows = pl.ds(pl.multiple_of(owner * block, block), block)
        slots = pl.ds(pl.multiple_of(cp * span + owner * block, block), block)
        feats = embed[rows, :].astype(F32)
        inv_rms = inverse_root(jnp.mean(feats * feats, axis=-1, keepdims=True) + NORM_EPS)
        act[rows, :] = (feats * inv_rms * gain[...]).astype(BF16)

        def step(j, carry):
            cols = pl.ds(pl.multiple_of(j * head, head), head)
            left = act[rows, :]
            query = jnp.dot(left, w_q[:, cols], preferred_element_type=F32)
            q_ref[rows, cols] = turn(query, cosine[rows, :], sine[rows, :]).astype(BF16)
            key = jnp.dot(left, w_k[:, cols], preferred_element_type=F32)
            k_ref[slots, cols] = turn(key, cosine[rows, :], sine[rows, :]).astype(BF16)
            v_ref[slots, cols] = jnp.dot(left, w_v[:, cols], preferred_element_type=F32).astype(BF16)
            return carry

        lax.fori_loop(0, w_q.shape[1] // head, step, 0)
        for ref in (k_ref, v_ref):
            slot = len(sent)
            copy = pltpu.make_async_remote_copy(
                src_ref=ref.at[slots], dst_ref=ref.at[slots], send_sem=kv_sems.at[0, slot], recv_sem=kv_sems.at[1, slot],
                device_id={"cp": 1 - cp}, device_id_type=MESH)
            copy.start()
            sent.append(copy)

    tp_exchange(compute, done, embed, part, recv1, recv2, sems)
    for copy in sent:
        copy.wait_recv()
    for copy in sent:
        copy.wait_send()


def embed_qkv(picked, gain, w_q, w_k, w_v, cosine, sine, cp_count, collective_id):
    span, width = picked.shape
    cols = w_q.shape[1]
    return pl.pallas_call(
        embed_kernel,
        out_shape=[jax.ShapeDtypeStruct(shape, BF16) for shape in (
            (span, width), (span, width), (span, cols), (span * cp_count, cols), (span * cp_count, cols))],
        in_specs=[VMEM_SPEC] * 7,
        out_specs=[VMEM_SPEC] * 5,
        scratch_shapes=exchange_scratch(span, width, BF16) + [pltpu.SemaphoreType.DMA((2, 8))],
        compiler_params=comm_params(collective_id),
        cost_estimate=EXCHANGE_COST,
        name="embed_qkv",
    )(picked, gain, w_q, w_k, w_v, cosine, sine)


def grad_b_kernel(d_gate, d_up, w_gate, w_up, out, part, recv1, recv2, sems):
    enter(neighbours()[1:3])
    tp_exchange(product_into(part, (d_gate, d_up), (w_gate, w_up), NN), lambda owner: None, out, part, recv1, recv2, sems)


def grad_b(d_gate, d_up, w_gate_t, w_up_t, collective_id):
    span, width = d_gate.shape[0], w_gate_t.shape[1]
    return pl.pallas_call(
        grad_b_kernel,
        out_shape=jax.ShapeDtypeStruct((span, width), BF16),
        in_specs=[VMEM_SPEC] * 4,
        out_specs=VMEM_SPEC,
        scratch_shapes=exchange_scratch(span, width, F32),
        compiler_params=comm_params(collective_id),
        cost_estimate=EXCHANGE_COST,
        name="grad_b",
    )(d_gate, d_up, w_gate_t, w_up_t)


def grad_a_kernel(
    d_q, d_k_all, d_v_all, w_q, w_k, w_v, cosine, sine, embed, gain, d_resid,
    d_embed, grad_gain, d_k, d_v, out, resid, recv_k, recv_v, part, recv1, recv2, sems, kv_sems, row_sems):
    span = d_q.shape[0]
    block = part.shape[2]
    head = cosine.shape[1]
    me, x_peer, y_peer, diag = neighbours()
    cp = lax.axis_index("cp")
    barrier = pltpu.get_barrier_semaphore()
    for peer in ({"tp": x_peer}, {"tp": y_peer}, {"cp": 1 - cp}):
        pl.semaphore_signal(barrier, inc=1, device_id=peer, device_id_type=MESH)
    pl.semaphore_wait(barrier, 3)
    load = pltpu.make_async_copy(d_resid, resid, row_sems.at[0, 0])
    load.start()
    order = (diag, x_peer, y_peer, me)
    copies = []
    for place, owner in enumerate(order):
        rows = pl.ds(pl.multiple_of(owner * block, block), block)
        theirs = pl.ds(pl.multiple_of((1 - cp) * span + owner * block, block), block)
        for which, (source, target) in enumerate(((d_k_all, recv_k), (d_v_all, recv_v))):
            slot = 2 * place + which
            copy = pltpu.make_async_remote_copy(
                src_ref=source.at[theirs], dst_ref=target.at[rows], send_sem=kv_sems.at[0, slot], recv_sem=kv_sems.at[1, slot],
                device_id={"cp": 1 - cp}, device_id_type=MESH)
            copy.start()
            copies.append(copy)
    product = product_into(part, (d_q, d_k, d_v), (w_q, w_k, w_v), NT)
    ready = []

    def prepare(place):
        owner = order[place]
        copies[2 * place].wait_recv()
        copies[2 * place + 1].wait_recv()
        rows = pl.ds(pl.multiple_of(owner * block, block), block)
        ours = pl.ds(pl.multiple_of(cp * span + owner * block, block), block)

        def step(j, carry):
            cols = pl.ds(pl.multiple_of(j * head, head), head)
            total = (d_k_all[ours, cols] + recv_k[rows, cols]).astype(BF16).astype(F32)
            d_k[rows, cols] = turn(total, cosine[rows, :], -sine[rows, :]).astype(BF16)
            d_v[rows, cols] = (d_v_all[ours, cols] + recv_v[rows, cols]).astype(BF16)
            return carry

        lax.fori_loop(0, d_q.shape[1] // head, step, 0)
        ready.append(place)

    calls = []

    def compute(side, owner):
        turn_no = len(calls)
        calls.append(side)
        if turn_no == 0:
            prepare(0)
        elif turn_no == 2:
            prepare(1)
        elif turn_no == 3:
            prepare(2)
        elif turn_no == 6:
            prepare(3)
        product(side, owner)

    grad_gain[...] = jnp.zeros_like(grad_gain)
    local, shared = [], []

    def done(owner):
        if not local:
            load.wait()
        rows = pl.ds(pl.multiple_of(owner * block, block), block)
        slots = pl.ds(pl.multiple_of(cp * span + owner * block, block), block)
        feats = embed[rows, :].astype(F32)
        inv_rms = inverse_root(jnp.mean(feats * feats, axis=-1, keepdims=True) + NORM_EPS)
        normed = feats * inv_rms
        d_act = out[rows, :].astype(F32)
        grad_gain[...] = grad_gain[...] + jnp.sum(d_act * normed, axis=0, keepdims=True)
        resid[rows, :] = resid[rows, :] + rms_back(d_act * gain[...], normed, inv_rms)
        slot = 1 + len(local)
        copy = pltpu.make_async_copy(resid.at[rows], d_embed.at[slots], row_sems.at[0, slot])
        copy.start()
        local.append(copy)
        copy = pltpu.make_async_remote_copy(
            src_ref=resid.at[rows], dst_ref=d_embed.at[slots], send_sem=row_sems.at[1, slot], recv_sem=row_sems.at[2, slot],
            device_id={"cp": 1 - cp}, device_id_type=MESH)
        copy.start()
        shared.append(copy)

    tp_exchange(compute, done, out, part, recv1, recv2, sems)
    for copy in local:
        copy.wait()
    for copy in shared:
        copy.wait_recv()
    for copy in copies + shared:
        copy.wait_send()


def grad_a(d_q, d_k_all, d_v_all, w_q, w_k, w_v, cosine, sine, embed, gain, d_resid, cp_count, collective_id):
    span, width = d_q.shape[0], w_q.shape[0]
    cols = d_q.shape[1]
    hbm = pl.BlockSpec(memory_space=pl.ANY)
    return pl.pallas_call(
        grad_a_kernel,
        out_shape=[
            jax.ShapeDtypeStruct((span * cp_count, width), F32), jax.ShapeDtypeStruct((1, width), F32),
            jax.ShapeDtypeStruct((span, cols), BF16), jax.ShapeDtypeStruct((span, cols), BF16)],
        in_specs=[VMEM_SPEC] * 10 + [hbm],
        out_specs=[hbm] + [VMEM_SPEC] * 3,
        scratch_shapes=[pltpu.VMEM((span, width), BF16), pltpu.VMEM((span, width), F32)] + [pltpu.VMEM((span, cols), F32)] * 2
        + exchange_scratch(span, width, F32) + [pltpu.SemaphoreType.DMA((2, 8)), pltpu.SemaphoreType.DMA((3, 5))],
        compiler_params=comm_params(collective_id),
        cost_estimate=EXCHANGE_COST,
        name="grad_a",
    )(d_q, d_k_all, d_v_all, w_q, w_k, w_v, cosine, sine, embed, gain, d_resid)


Q_TILE = 256


def key_row(chunk, size):
    return pl.multiple_of(jnp.where(chunk < 2, 2 * chunk, 7 - 2 * chunk) * size, size)


def query_plan(i, size, pos_smem):
    cp = lax.axis_index("cp")
    per_block = size // Q_TILE
    seq_block = jnp.where(i < per_block, cp, 3 - cp)
    start = seq_block * size + lax.rem(i, per_block) * Q_TILE
    low = jnp.maximum(start - pos_smem[i * Q_TILE], 0) // size
    return start, low, seq_block + 1


def distance(size):
    return lax.broadcasted_iota(jnp.int32, (Q_TILE, size), 0) - lax.broadcasted_iota(jnp.int32, (Q_TILE, size), 1)


def attend_kernel(pos_smem, q_ref, k_ref, v_ref, pos_ref, o_ref, lse_ref, held):
    size = held.shape[2]
    head = q_ref.shape[1]
    scale = head ** -0.5

    def block(i, carry):
        start, low, high = query_plan(i, size, pos_smem)
        rows = pl.ds(pl.multiple_of(i * Q_TILE, Q_TILE), Q_TILE)
        query = q_ref[rows, :]
        back = pos_ref[rows, :]

        def score(c, top):
            keys = k_ref[pl.ds(key_row(c, size), size), :]
            scores = lax.dot_general(query, keys, NT, preferred_element_type=F32) * scale
            gap = distance(size) + (start - c * size)
            scores = jnp.where((gap >= 0) & (gap <= back), scores, NEG_BIG)
            held[c] = scores
            return jnp.maximum(top, jnp.max(scores, axis=1, keepdims=True))

        top = lax.fori_loop(low, high, score, jnp.full((Q_TILE, 1), NEG_BIG, F32))

        def expo(c, total):
            prob = jnp.exp(held[c] - top)
            held[c] = prob
            return total + jnp.sum(prob, axis=1, keepdims=True)

        total = lax.fori_loop(low, high, expo, jnp.zeros((Q_TILE, 1), F32))
        share = 1.0 / total

        def gather(c, acc):
            prob = (held[c] * share).astype(BF16)
            values = v_ref[pl.ds(key_row(c, size), size), :]
            return acc + jnp.dot(prob, values, preferred_element_type=F32)

        acc = lax.fori_loop(low, high, gather, jnp.zeros((Q_TILE, head), F32))
        o_ref[rows, :] = acc.astype(BF16)
        lse_ref[rows, :] = jnp.broadcast_to(top + jnp.log(total), (Q_TILE, head))
        return carry

    lax.fori_loop(0, q_ref.shape[0] // Q_TILE, block, 0)


def attend_back_kernel(pos_smem, q_ref, k_ref, v_ref, do_ref, lse_ref, pos_ref, cosine, sine, dq_ref, dk_ref, dv_ref, held_p, held_d):
    size = held_p.shape[2]
    head = q_ref.shape[1]
    scale = head ** -0.5
    dk_ref[...] = jnp.zeros_like(dk_ref)
    dv_ref[...] = jnp.zeros_like(dv_ref)
    over_rows = (((0,), (0,)), ((), ()))

    def block(i, carry):
        start, low, high = query_plan(i, size, pos_smem)
        rows = pl.ds(pl.multiple_of(i * Q_TILE, Q_TILE), Q_TILE)
        query = q_ref[rows, :]
        d_out = do_ref[rows, :]
        lse = lse_ref[rows, :][:, :1]
        back = pos_ref[rows, :]

        def probs(c, total):
            place = pl.ds(key_row(c, size), size)
            scores = lax.dot_general(query, k_ref[place, :], NT, preferred_element_type=F32) * scale
            gap = distance(size) + (start - c * size)
            prob = jnp.where((gap >= 0) & (gap <= back), jnp.exp(scores - lse), 0.0)
            d_prob = to_bf16(lax.dot_general(d_out, v_ref[place, :], NT, preferred_element_type=F32))
            held_p[c] = prob
            held_d[c] = d_prob
            return total + jnp.sum(prob * d_prob, axis=1, keepdims=True)

        mean = lax.fori_loop(low, high, probs, jnp.zeros((Q_TILE, 1), F32))

        def grads(c, acc):
            place = pl.ds(key_row(c, size), size)
            prob = held_p[c]
            d_score = (prob * (held_d[c] - mean) * scale).astype(BF16)
            dk_ref[place, :] = dk_ref[place, :] + lax.dot_general(d_score, query, over_rows, preferred_element_type=F32)
            dv_ref[place, :] = dv_ref[place, :] + lax.dot_general(prob.astype(BF16), d_out, over_rows, preferred_element_type=F32)
            return acc + jnp.dot(d_score, k_ref[place, :], preferred_element_type=F32)

        d_query = lax.fori_loop(low, high, grads, jnp.zeros((Q_TILE, head), F32))
        dq_ref[rows, :] = turn(to_bf16(d_query), cosine[rows, :], -sine[rows, :]).astype(BF16)
        return carry

    lax.fori_loop(0, q_ref.shape[0] // Q_TILE, block, 0)


def attention(query, key_all, value_all, pos, head):
    span, cols = query.shape
    total = key_all.shape[0]
    size = total // 4
    own = pl.BlockSpec((span, head), lambda h, *_: (0, h))
    full = pl.BlockSpec((total, head), lambda h, *_: (0, h))
    pos_spec = pl.BlockSpec((span, 1), lambda h, *_: (0, 0))
    flops = 4 * span * total * cols
    return pl.pallas_call(
        attend_kernel,
        grid_spec=pltpu.PrefetchScalarGridSpec(
            num_scalar_prefetch=1, grid=(cols // head,), in_specs=[own, full, full, pos_spec], out_specs=[own, own],
            scratch_shapes=[pltpu.VMEM((4, Q_TILE, size), F32)]),
        out_shape=[jax.ShapeDtypeStruct((span, cols), BF16), jax.ShapeDtypeStruct((span, cols), F32)],
        cost_estimate=pl.CostEstimate(flops=flops, bytes_accessed=8 * total * cols, transcendentals=0),
        compiler_params=pltpu.CompilerParams(vmem_limit_bytes=VMEM_LIMIT // 2),
        name="attention",
    )(pos, query, key_all, value_all, pos[:, None])


def attention_back(query, key_all, value_all, d_att, lse, pos, cosine, sine):
    span, cols = query.shape
    head = cosine.shape[1]
    total = key_all.shape[0]
    size = total // 4
    own = pl.BlockSpec((span, head), lambda h, *_: (0, h))
    full = pl.BlockSpec((total, head), lambda h, *_: (0, h))
    same = pl.BlockSpec((span, head), lambda h, *_: (0, 0))
    pos_spec = pl.BlockSpec((span, 1), lambda h, *_: (0, 0))
    flops = 10 * span * total * cols
    return pl.pallas_call(
        attend_back_kernel,
        grid_spec=pltpu.PrefetchScalarGridSpec(
            num_scalar_prefetch=1, grid=(cols // head,),
            in_specs=[own, full, full, own, own, pos_spec, same, same], out_specs=[own, full, full],
            scratch_shapes=[pltpu.VMEM((4, Q_TILE, size), F32)] * 2),
        out_shape=[jax.ShapeDtypeStruct((span, cols), BF16)] + [jax.ShapeDtypeStruct((total, cols), F32)] * 2,
        cost_estimate=pl.CostEstimate(flops=flops, bytes_accessed=16 * total * cols, transcendentals=0),
        compiler_params=pltpu.CompilerParams(vmem_limit_bytes=VMEM_LIMIT // 2),
        name="attention_back",
    )(pos, query, key_all, value_all, d_att, lse, pos[:, None], cosine, sine)


ROW_TILE = 200


def table_kernel(start, order, ids, source, out_ref, grads, sem):
    step = pl.program_id(0)

    @pl.when(step == 0)
    def _():
        copy = pltpu.make_async_copy(source, grads, sem)
        copy.start()
        copy.wait()

    out_ref[...] = jnp.zeros_like(out_ref)
    base = step * out_ref.shape[0]

    def add(i, carry):
        row = pl.ds(ids[i] - base, 1)
        out_ref[row, :] = out_ref[row, :] + grads[pl.ds(order[i], 1), :]
        return carry

    lax.fori_loop(start[step], start[step + 1], add, 0)


def table_grad(ids, order, start, source, rows):
    total, width = source.shape
    tiles = rows // ROW_TILE
    return pl.pallas_call(
        table_kernel,
        grid_spec=pltpu.PrefetchScalarGridSpec(
            num_scalar_prefetch=3, grid=(tiles,), in_specs=[pl.BlockSpec(memory_space=pl.ANY)],
            out_specs=pl.BlockSpec((ROW_TILE, width), lambda i, *_: (i, 0)),
            scratch_shapes=[pltpu.VMEM((total, width), F32), pltpu.SemaphoreType.DMA]),
        out_shape=jax.ShapeDtypeStruct((rows, width), F32),
        cost_estimate=pl.CostEstimate(flops=3 * 10**10, bytes_accessed=4 * rows * width, transcendentals=0),
        compiler_params=pltpu.CompilerParams(vmem_limit_bytes=VMEM_LIMIT // 2),
        name="table_grad",
    )(start, order, ids, source)


def out_proj_kernel(att_ref, w_mine, w_other, embed_ref, res_ref, slots, sems):
    me, x_peer, y_peer, diag = neighbours()
    peers = (x_peer, y_peer)
    enter(peers)
    width = att_ref.shape[1]
    half = att_ref.shape[0] // 2
    sides = [pl.ds(0, half), pl.ds(half, half)]

    cp = lax.axis_index("cp")
    part = w_mine.shape[1]
    tile = 256

    def multiply(block, owner, initial):
        rows = pl.ds(pl.multiple_of(owner * width, width), width)
        for w_ref, base in ((w_mine, cp), (w_other, 1 - cp)):

            def step(j, carry):
                cols = pl.ds(pl.multiple_of(base * part + j * tile, tile), tile)
                term = jnp.dot(block[...], w_ref[rows, pl.ds(pl.multiple_of(j * tile, tile), tile)], preferred_element_type=F32)
                before = embed_ref[:, cols].astype(F32) if initial else res_ref[:, cols]
                res_ref[:, cols] = before + term
                return carry

            lax.fori_loop(0, part // tile, step, 0)

    near = []
    for side in range(2):
        copy = remote(att_ref.at[sides[side]], slots.at[me, sides[side]], sems, side, peers[side])
        copy.start()
        near.append(copy)
    far = []
    for side in range(2):
        copy = remote(att_ref.at[sides[side]], slots.at[me, sides[side]], sems, 2 + side, peers[1 - side])
        copy.start()
        far.append(copy)
    multiply(att_ref, me, True)
    last = []
    for side in range(2):
        near[side].wait_recv()
        owner = peers[side]
        copy = remote(slots.at[owner, sides[side]], slots.at[owner, sides[side]], sems, 4 + side, peers[1 - side])
        copy.start()
        last.append(copy)
    for side in range(2):
        far[side].wait_recv()
    for side in range(2):
        multiply(slots.at[peers[side]], peers[side], False)
    for side in range(2):
        last[side].wait_recv()
    multiply(slots.at[diag], diag, False)
    for copy in near + far + last:
        copy.wait_send()


def out_proj(attended, w_mine, w_other, embed, collective_id):
    span, width = attended.shape
    vmem = pl.BlockSpec(memory_space=pltpu.VMEM)
    return pl.pallas_call(
        out_proj_kernel,
        out_shape=jax.ShapeDtypeStruct(embed.shape, F32),
        in_specs=[vmem] * 4,
        out_specs=vmem,
        scratch_shapes=[pltpu.VMEM((4, span, width), BF16), pltpu.SemaphoreType.DMA((2, 6))],
        compiler_params=pltpu.CompilerParams(
            collective_id=collective_id, has_side_effects=True, vmem_limit_bytes=VMEM_LIMIT),
        cost_estimate=EXCHANGE_COST,
        name="out_proj",
    )(attended, w_mine, w_other, embed)


def solution(mesh):
    cp_count = mesh.shape["cp"]

    def device_step(tokens, pos, doc_id, dy, table, w_q, w_k, w_v, w_o, w_gate, w_up, w_down, gain_one, gain_two, inv_freq):
        span = tokens.shape[0]
        rows = table.shape[0]
        head_dim = 2 * inv_freq.shape[0]
        tp_rank = lax.axis_index("tp")
        gain_a = gain_one.astype(F32)
        gain_b = gain_two.astype(F32)
        swap = [(0, 1), (1, 0)]

        local_ids = tokens - tp_rank * rows
        owned = (local_ids >= 0) & (local_ids < rows)
        safe_ids = jnp.where(owned, local_ids, jnp.arange(span, dtype=jnp.int32) % rows)
        picked = jnp.where(owned[:, None], jnp.take(table, safe_ids, axis=0), jnp.zeros((), BF16))
        half_width = w_o.shape[1] // cp_count
        w_o_half = lax.dynamic_slice_in_dim(w_o, lax.axis_index("cp") * half_width, half_width, axis=1)
        w_o_mine = lax.all_gather(w_o_half, "tp", axis=0, tiled=True)
        w_o_other = lax.ppermute(w_o_mine, "cp", swap)
        all_ids = lax.all_gather(tokens, "cp", axis=0, tiled=True) - tp_rank * rows
        all_ids = jnp.where((all_ids >= 0) & (all_ids < rows), all_ids, rows)
        ids, order = lax.sort((all_ids, jnp.arange(all_ids.shape[0], dtype=jnp.int32)), num_keys=1, is_stable=True)
        edges = jnp.arange(rows // ROW_TILE + 1, dtype=jnp.int32) * ROW_TILE
        starts = jnp.sum((all_ids[None, :] < edges[:, None]).astype(jnp.int32), axis=1)
        angle = pos.astype(F32)[:, None] * inv_freq
        cosine, sine = jnp.cos(angle), jnp.sin(angle)
        cosine = jnp.concatenate([cosine, cosine], axis=1)
        sine = jnp.concatenate([-sine, sine], axis=1)
        embed_b, act_a, query, key_all, value_all = embed_qkv(picked, gain_a[None, :], w_q, w_k, w_v, cosine, sine, cp_count, 0)
        attended, lse = attention(query, key_all, value_all, pos, head_dim)
        residual = out_proj(attended, w_o_mine, w_o_other, embed_b, 1)
        normed_b, inv_b = rms_stats(residual)
        act_b = (normed_b * gain_b).astype(BF16)
        gate = jnp.dot(act_b, w_gate, preferred_element_type=F32)
        up_val = jnp.dot(act_b, w_up, preferred_element_type=F32)
        gate_sig = jax.nn.sigmoid(gate)
        hidden = (gate * gate_sig * up_val).astype(BF16)
        d_hidden = to_bf16(jnp.einsum("td,fd->tf", dy, w_down, preferred_element_type=F32))
        d_gate = (d_hidden * up_val * gate_sig * (1.0 + gate * (1.0 - gate_sig))).astype(BF16)
        d_up = (d_hidden * gate * gate_sig).astype(BF16)
        d_act_b = grad_b(d_gate, d_up, w_gate.T, w_up.T, 2)

        hidden, d_act_b = lax.optimization_barrier((hidden, d_act_b))
        out_part = jnp.dot(hidden, w_down, preferred_element_type=F32)
        out_mine = lax.psum_scatter(out_part, "tp", scatter_dimension=0, tiled=True)

        grad_down = jnp.einsum("tf,td->fd", hidden, dy, preferred_element_type=F32)
        grad_gate = jnp.einsum("tf,td->fd", d_gate, act_b, preferred_element_type=F32)
        grad_up = jnp.einsum("tf,td->fd", d_up, act_b, preferred_element_type=F32)
        d_act_b = d_act_b.astype(F32)
        grad_gain_b = jnp.sum(d_act_b * normed_b, axis=0)
        d_resid = dy.astype(F32) + rms_back(d_act_b * gain_b, normed_b, inv_b)
        d_resid_b = d_resid.astype(BF16)
        grad_out = jnp.einsum("tc,td->cd", attended, d_resid_b, preferred_element_type=F32)
        d_att = jnp.einsum("td,cd->tc", d_resid_b, w_o, preferred_element_type=F32).astype(BF16)
        d_q_pre, d_key_all, d_value_all = attention_back(query, key_all, value_all, d_att, lse, pos, cosine, sine)
        out_mine, d_q_pre, grad_gate, grad_up, grad_down = lax.optimization_barrier(
            (out_mine, d_q_pre, grad_gate, grad_up, grad_down))
        grad_gate, grad_up, grad_down = lax.psum((grad_gate, grad_up, grad_down), "cp")
        d_embed, grad_gain_a, d_k_pre, d_v_pre = grad_a(
            d_q_pre, d_key_all, d_value_all, w_q, w_k, w_v, cosine, sine, embed_b, gain_a[None, :], d_resid, cp_count, 3)
        grad_gain_a = grad_gain_a[0]
        out_mine, d_embed = lax.optimization_barrier((out_mine, d_embed))
        res_mine = lax.dynamic_slice_in_dim(residual, tp_rank * (span // 4), span // 4, axis=0)
        layer_out = lax.all_gather((out_mine + res_mine).astype(BF16), "tp", axis=0, tiled=True)
        grad_table = table_grad(ids, order, starts, d_embed, rows)
        grad_q = jnp.einsum("td,tc->dc", act_a, d_q_pre, preferred_element_type=F32)
        grad_k = jnp.einsum("td,tc->dc", act_a, d_k_pre, preferred_element_type=F32)
        grad_v = jnp.einsum("td,tc->dc", act_a, d_v_pre, preferred_element_type=F32)
        (grad_q, grad_k, grad_v, grad_out), (grad_gate, grad_up, grad_down) = lax.optimization_barrier(
            ((grad_q, grad_k, grad_v, grad_out), (grad_gate, grad_up, grad_down)))
        att_grads = lax.psum((grad_q, grad_k, grad_v, grad_out), "cp")
        gains = lax.psum((grad_gain_a, grad_gain_b), "cp")
        return (layer_out, grad_table) + tuple(att_grads) + (grad_gate.T, grad_up.T, grad_down) + tuple(gains)

    col_spec = P(None, "tp")
    row_spec = P("tp", None)
    tok_spec = P("cp")
    rep_spec = P(None)
    in_specs = (tok_spec, tok_spec, tok_spec, P("cp", None), row_spec, col_spec, col_spec, col_spec, row_spec, col_spec, col_spec, row_spec, rep_spec, rep_spec, rep_spec)
    out_specs = (P("cp", None), row_spec, col_spec, col_spec, col_spec, row_spec, col_spec, col_spec, row_spec, rep_spec, rep_spec)
    return jax.shard_map(device_step, mesh=mesh, in_specs=in_specs, out_specs=out_specs, check_vma=False)
```

time: 962 us -> 773 us (0.80)
  other arithmetic: 208 us -> 33.3 us
  matrix products: 210 us -> 96.4 us
  Pallas kernels: 368 us -> 470 us
  local copies, waits for them, and re-layouts: 119 us -> 95.6 us
  waiting for transfers between devices: 26.3 us -> 47.8 us
    dot_general x14 -> x5, matrix products: 154 us -> 40.3 us  [the longest x1 11.5 us: device_step(): out_part = jnp.dot(hidden, w_down, preferred_element_type=F32)]
    pallas_call x3 -> x6, Pallas kernels: 319 us -> 421 us  [the longest x1 128 us: grad_a(): pl.pallas_call(grad_a_kernel, out_shape=[jax.ShapeDtypeStruct((span * cp_...]
    scatter-add x3 -> x0, other arithmetic: 89.4 us -> none  [device_step(): grad_table = jax.ops.segment_sum(all_grads, all_ids, num_segments=rows)]
    another operation x3 -> x0, other arithmetic: 32.4 us -> none
    psum x1, waiting for transfers between devices: 0.01 us -> 23 us  [device_step(): att_grads = lax.psum((grad_q, grad_k, grad_v, grad_out), 'cp')]
    reduce_sum x2 -> x1, other arithmetic: 19.5 us -> 0.21 us  [device_step(): jnp.sum((all_ids[None, :] < edges[:, None]).astype(jnp.int32), axis=1)]
    select_n x1 -> x0, other arithmetic: 17.5 us -> none  [device_step(): jnp.where(even, jnp.concatenate([d_embed, d_embed_other]), jnp.concatenat...]
    ppermute x2 -> x1, waiting for transfers between devices: 12.7 us -> 0.01 us  [device_step(): w_o_other = lax.ppermute(w_o_mine, 'cp', swap)]
  transfers between devices with their start and end apart: 10 -> 6, of which waited for: 3 -> 3; matrix products, arithmetic and copies ran while one was open for 42% -> 15% of each run, Pallas kernels for 12% -> 40%
where the time goes in v2:
time: 773 us; the launch traced here: 764 us
  Pallas kernels  470 us (61%)
  matrix products  96.4 us (12%)
  local copies, waits for them, and re-layouts  95.6 us (12%)
  waiting for transfers between devices  47.8 us (6%)
  other arithmetic  33.3 us (4%)
  between operations  14.5 us (2%)
    pallas_call x1, Pallas kernels, grad_a(): pl.pallas_call(grad_a_kernel, out_shape=[jax.ShapeDtypeStruct((span * cp_...  128 us
    pallas_call x1, Pallas kernels, grad_b(): pl.pallas_call(grad_b_kernel, out_shape=jax.ShapeDtypeStruct((span, width...  116 us
    pallas_call x1, Pallas kernels, embed_qkv(): pl.pallas_call(embed_kernel, out_shape=[jax.ShapeDtypeStruct(shape, BF16)...  88.6 us
    unnamed x104, local copies, waits for them, and re-layouts  70 us
    pallas_call x1, Pallas kernels, out_proj(): pl.pallas_call(out_proj_kernel, out_shape=jax.ShapeDtypeStruct(embed.shap...  48.6 us
    pallas_call x1, Pallas kernels, table_grad(): pl.pallas_call(table_kernel, grid_spec=pltpu.PrefetchScalarGridSpec(num_s...  38.1 us
    pallas_call x1, Pallas kernels, attention_back(): pl.pallas_call(attend_back_kernel, grid_spec=pltpu.PrefetchScalarGridSpec...  27.9 us
    gather x1, local copies, waits for them, and re-layouts, device_step(): jnp.take(table, safe_ids, axis=0)  24.3 us
  transfers between devices with their start and end apart: 6, of which 3 were waited for; matrix products, arithmetic and copies ran while one was open for 15% of the time, Pallas kernels for 40%

profile of v2, /device:TPU:0, one launch (start us, length us, event | category | flops | bytes accessed | tf_op | source)
XLA Modules:
  0.0 764.0 jit_solution(10762697297486720586)
XLA Ops:
  12.6 24.3 %gather_fusion = bf16[1024,2048]{1,0:T(8,128)(2,1)} fusion(bf16[8000,2048]{1,0:T(8,128)(2,1)} %param.18, s32[1024]{0:T(1024)S(1)} %fusion.19), kind=kCustom, calls=%fused_computation | custom fusion | bytes 8392704 | tf_op jit(solution)/shard_map/jit(_take)/gather | solution.py:631
  42.7 17.1 %all-gather.3.cloned.1.call-done.w_mine = bf16[2048,1024]{1,0:T(8,128)(2,1)} async-done(((bf16[512,1024]{1,0:T(8,128)(2,1)}), bf16[2048,1024]{1,0:T(8,128)(2,1)}) %all-gather.3.cloned.1.call-update) | async-done | bytes 4194320 | tf_op jit(solution)/shard_map/all_gather | solution.py:634
  59.9 88.6 %embed_qkv.1 = (bf16[1024,2048]{1,0:T(8,128)(2,1)}, bf16[1024,2048]{1,0:T(8,128)(2,1)}, bf16[1024,512]{1,0:T(8,128)(2,1)}, bf16[2048,512]{1,0:T(8,128)(2,1)}, bf16[2048,512]{1,0:T(8,128)(2,1)}) custom-call(bf16[1024,2048]{1,0:T(8,128)(2,1)} %select_select_fusion.picked, f32[1,2048]{1,0:T(1,128)} %bitcast.32, bf16[2048,512]{1,0:T(8,128)(2,1)} %w_q.3, ...), custom_call_target="tpu_custom_call" | custom-call | flops 99999997952 | bytes 100000000 | tf_op jit(solution)/shard_map/embed_qkv/pallas_call | solution.py:214
  153.3 21.7 %attention.1 = (bf16[1024,512]{1,0:T(8,128)(2,1)S(1)}, f32[1024,512]{1,0:T(8,128)S(1)}) custom-call(s32[1024]{0:T(1024)S(1)} %copy-done.7, bf16[1024,512]{1,0:T(8,128)(2,1)S(1)} %copy-done.18, bf16[2048,512]{1,0:T(8,128)(2,1)S(1)} %copy-done.11, bf16[2048,512]{1,0:T(8,128)(2,1)S(1)} %copy-done.13, s32[1024,1]{1,0:T(8,128)S(1)} %copy.50.pos_ref), custom_call_target="tpu_custom_call" | custom-call | flops 4294967296 | bytes 8388608 | tf_op jit(solution)/shard_map/attention/pallas_call | solution.py:472
  176.1 11.6 %convolution_convert_fusion = bf16[1024,1376]{1,0:T(8,128)(2,1)} fusion(bf16[1024,2048]{1,0:T(8,128)(2,1)S(1)} %copy-done.32, bf16[1376,2048]{1,0:T(8,128)(2,1)} %param.25), kind=kOutput, calls=%fused_computation.21 | convolution fusion | flops 5772771328 | bytes 12648448 | tf_op jit(solution)/shard_map/td,fd->tf/dot_general | solution.py:654
  187.7 48.6 %out_proj.1 = f32[1024,2048]{1,0:T(8,128)} custom-call(bf16[1024,512]{1,0:T(8,128)(2,1)} %copy-done.1, bf16[2048,1024]{1,0:T(8,128)(2,1)} %all-gather.3.cloned.1.call-done.w_mine, bf16[2048,1024]{1,0:T(8,128)(2,1)} %collective-permute-done.w_other, bf16[1024,2048]{1,0:T(8,128)(2,1)} %get-tuple-element.47.embed_ref.embed), custom_call_target="tpu_custom_call" | custom-call | flops 99999997952 | bytes 100000000 | tf_op jit(solution)/shard_map/out_proj/pallas_call | solution.py:603
  236.3 4.1 multiply_reduce_fusion
  243.8 8.5 %fusion.20 = f32[1024,1376]{1,0:T(8,128)} fusion(bf16[1024,2048]{1,0:T(8,128)(2,1)S(1)} %multiply_convert_fusion, bf16[2048,1376]{0,1:T(8,128)(2,1)S(1)} %bitcast.37), kind=kOutput, calls=%fused_computation.43 | convolution fusion | flops 5771362304 | bytes 15466496 | tf_op jit(solution)/shard_map/dot_general | solution.py:650
  252.3 15.0 %fusion.8 = (bf16[1024,1376]{1,0:T(8,128)(2,1)}, bf16[1024,1376]{1,0:T(8,128)(2,1)}, bf16[1024,1376]{1,0:T(8,128)(2,1)}) fusion(bf16[1024,1376]{1,0:T(8,128)(2,1)} %convolution_convert_fusion, f32[1024,1376]{1,0:T(8,128)} %fusion.20, bf16[1024,2048]{1,0:T(8,128)(2,1)S(1)} %multiply_convert_fusion, bf16[2048,1376]{0,1:T(8,128)(2,1)} %param.24), kind=kOutput, calls=%fused_computation.15 | convolution fusion | flops 5795315712 | bytes 26738688 | tf_op jit(solution)/shard_map/dot_general | solution.py:651
  267.3 116.4 %grad_b.1 = bf16[1024,2048]{1,0:T(8,128)(2,1)} custom-call(bf16[1024,1376]{1,0:T(8,128)(2,1)} %get-tuple-element.86.d_gate, bf16[1024,1376]{1,0:T(8,128)(2,1)} %get-tuple-element.88.d_up, bf16[1376,2048]{1,0:T(8,128)(2,1)} %bitcast.35, bf16[1376,2048]{1,0:T(8,128)(2,1)} %bitcast.38), custom_call_target="tpu_custom_call" | custom-call | flops 99999997952 | bytes 100000000 | tf_op jit(solution)/shard_map/grad_b/pallas_call | solution.py:234
  383.7 11.5 %fusion.21 = f32[1024,2048]{1,0:T(8,128)} fusion(bf16[1024,1376]{1,0:T(8,128)(2,1)} %get-tuple-element.48, bf16[1376,2048]{1,0:T(8,128)(2,1)} %param.25), kind=kOutput, calls=%fused_computation.44 | convolution fusion | flops 5771362304 | bytes 16842752 | tf_op jit(solution)/shard_map/dot_general | solution.py:660
  395.4 6.9 fusion.5
  402.4 4.8 fusion.4.d_resid
  413.9 27.9 %attention_back.1 = (bf16[1024,512]{1,0:T(8,128)(2,1)S(1)}, f32[2048,512]{1,0:T(8,128)S(1)}, f32[2048,512]{1,0:T(8,128)S(1)}) custom-call(s32[1024]{0:T(1024)S(1)} %copy-done.8, bf16[1024,512]{1,0:T(8,128)(2,1)S(1)} %copy-done.19, bf16[2048,512]{1,0:T(8,128)(2,1)S(1)} %copy-done.12, bf16[2048,512]{1,0:T(8,128)(2,1)S(1)} %copy-done.14, ...), custom_call_target="tpu_custom_call" | custom-call | flops 10737418240 | bytes 16777216 | tf_op jit(solution)/shard_map/attention_back/pallas_call | solution.py:494
  441.9 8.9 %fusion.24 = f32[1376,2048]{1,0:T(8,128)} fusion(bf16[1024,1376]{1,0:T(8,128)(2,1)S(1)} %copy-done.42, bf16[1024,2048]{1,0:T(8,128)(2,1)S(1)} %copy-done.33), kind=kOutput, calls=%fused_computation.47 | convolution fusion | flops 5771362304 | bytes 18284544 | tf_op jit(solution)/shard_map/tf,td->fd/dot_general | solution.py:663
  450.9 8.8 %fusion.23 = f32[1376,2048]{1,0:T(8,128)} fusion(bf16[1024,1376]{1,0:T(8,128)(2,1)S(1)} %copy-done.41, bf16[1024,2048]{1,0:T(8,128)(2,1)S(1)} %copy-done.27), kind=kOutput, calls=%fused_computation.46 | convolution fusion | flops 5771362304 | bytes 18284544 | tf_op jit(solution)/shard_map/tf,td->fd/dot_general | solution.py:665
  459.7 8.7 %fusion.22 = f32[1376,2048]{1,0:T(8,128)} fusion(bf16[1024,1376]{1,0:T(8,128)(2,1)S(1)} %copy-done.40, bf16[1024,2048]{1,0:T(8,128)(2,1)S(1)} %copy-done.27), kind=kOutput, calls=%fused_computation.45 | convolution fusion | flops 5771362304 | bytes 18284544 | tf_op jit(solution)/shard_map/tf,td->fd/dot_general | solution.py:664
  468.4 7.6 reduce-scatter.2.cloned.1.call-done
  476.1 128.5 %grad_a.1 = (f32[2048,2048]{1,0:T(8,128)}, f32[1,2048]{1,0:T(1,128)}, bf16[1024,512]{1,0:T(8,128)(2,1)}, bf16[1024,512]{1,0:T(8,128)(2,1)}) custom-call(bf16[1024,512]{1,0:T(8,128)(2,1)} %copy-done.9, f32[2048,512]{1,0:T(8,128)} %copy-done.20, f32[2048,512]{1,0:T(8,128)} %copy-done.21, bf16[2048,512]{1,0:T(8,128)(2,1)} %w_q.3, bf16[2048,512]{1,0:T(8,128)(2,1)} %w_k.3, ...), custom_call_target="tpu_custom_call" | custom-call | flops 99999997952 | bytes 100000000 | tf_op jit(solution)/shard_map/grad_a/pallas_call | solution.py:344
  608.4 7.9 %fusion.11 = f32[512,2048]{1,0:T(8,128)} fusion(bf16[1024,512]{1,0:T(8,128)(2,1)S(1)} %copy-done.2, f32[1024,2048]{1,0:T(8,128)} %copy-done.23), kind=kOutput, calls=%fused_computation.23 | convolution fusion | flops 2149580800 | bytes 13631488 | tf_op jit(solution)/shard_map/tc,td->cd/dot_general | solution.py:670
  616.3 4.4 fusion.25
  620.7 4.4 fusion.26
  625.1 4.4 fusion.27
  632.0 4.4 sort.15
  636.7 4.4 all-reduce
  641.0 5.8 copy-done.17
  646.8 38.1 %table_grad.1 = f32[8000,2048]{1,0:T(8,128)} custom-call(s32[41]{0:T(128)S(1)} %convert_reduce_fusion.start, s32[2048]{0:T(1024)S(1)} %get-tuple-element.58.order, s32[2048]{0:T(1024)S(1)} %get-tuple-element.59.ids, f32[2048,2048]{1,0:T(8,128)S(1)} %copy-done.17), custom_call_target="tpu_custom_call" | custom-call | flops 30000001024 | bytes 65536000 | tf_op jit(solution)/shard_map/table_grad/pallas_call | solution.py:533
  685.0 23.0 %all-reduce.6.cloned.1.call-done = (f32[2048,512]{1,0:T(8,128)}, f32[2048,512]{1,0:T(8,128)}, f32[2048,512]{1,0:T(8,128)}, f32[512,2048]{1,0:T(8,128)}) async-done(((f32[2048,512]{1,0:T(8,128)}, f32[2048,512]{1,0:T(8,128)}, f32[2048,512]{1,0:T(8,128)}, f32[512,2048]{1,0:T(8,128)}), (f32[2048,512]{1,0:T(8,128)}, f32[2048,512]{1,0:T(8,128)}, f32[2048,512]{1,0:T(8,128)}, ...) | async-done | bytes 16777232 | tf_op jit(solution)/shard_map/psum | solution.py:688
  707.9 4.9 copy.70
  726.0 10.4 %copy.75 = f32[2048,1376]{0,1:T(8,128)} copy(f32[2048,1376]{0,1:T(8,128)} %bitcast.31) | data formatting | bytes 22544384
  736.4 10.4 %copy.76 = f32[2048,1376]{0,1:T(8,128)} copy(f32[2048,1376]{0,1:T(8,128)} %bitcast.30) | data formatting | bytes 22544384
  746.8 10.4 %copy.77 = f32[1376,2048]{1,0:T(8,128)} copy(f32[1376,2048]{1,0:T(8,128)} %get-tuple-element.115) | data formatting | bytes 22544384
  (134 shorter events, 47.1 us)
Async XLA Ops:
  7.2 52.7 %all-gather.3.cloned.1.call-start = ((), (), s32[]{:S(2)}) async-start(), calls=%async_computation.1 | async-start | bytes 5242880 | tf_op jit(solution)/shard_map/all_gather | solution.py:634
  9.9 466.1 %reduce-scatter.2.cloned.1.call-start = ((), (), s32[]{:S(2)}) async-start(), calls=%async_computation.2 | async-start | bytes 10485760 | tf_op jit(solution)/shard_map/reduce_scatter | solution.py:661
  12.6 24.3 %copy-start.39 = (f32[64]{0:T(128)S(1)}, f32[64]{0:T(128)}, u32[]{:S(2)}) copy-start(f32[64]{0:T(128)} %param.28) | copy-start | bytes 772
  59.9 127.8 %collective-permute-start = (bf16[2048,1024]{1,0:T(8,128)(2,1)}, bf16[2048,1024]{1,0:T(8,128)(2,1)}, u32[]{:S(2)}, u32[]{:S(2)}) collective-permute-start(bf16[2048,1024]{1,0:T(8,128)(2,1)} %all-gather.3.cloned.1.call-done.w_mine), channel_id=1, source_target_pairs={{0,1},{1,0},{2,3},{3,2},{4,5},{5,4},{6,7},{7,6}} | collective-permute-start | bytes 12582920 | tf_op jit(solution)/shard_map/ppermute | solution.py:635
  59.9 88.6 %copy-start.38 = (bf16[2048]{0:T(1024)(128)(2,1)S(1)}, bf16[2048]{0:T(1024)(128)(2,1)}, u32[]{:S(2)}) copy-start(bf16[2048]{0:T(1024)(128)(2,1)} %param.27) | copy-start | bytes 12292
  59.9 88.6 %copy-start.7 = (s32[1024]{0:T(1024)S(1)}, s32[1024]{0:T(1024)}, u32[]{:S(2)}) copy-start(s32[1024]{0:T(1024)} %pos_smem.3) | copy-start | bytes 12292
  148.7 26.3 %copy-start.5 = (s32[1024,1]{1,0:T(8,128)}, s32[1024,1]{1,0:T(8,128)S(1)}, u32[]{:S(2)}) copy-start(s32[1024,1]{1,0:T(8,128)S(1)} %copy.50.pos_ref) | copy-start | bytes 12292
  153.3 22.7 %copy-start.32 = (bf16[1024,2048]{1,0:T(8,128)(2,1)S(1)}, bf16[1024,2048]{1,0:T(8,128)(2,1)}, u32[]{:S(2)}) copy-start(bf16[1024,2048]{1,0:T(8,128)(2,1)} %param.17) | copy-start | bytes 12582916
  176.1 11.6 %copy-start.15 = (f32[1024,512]{1,0:T(8,128)}, f32[1024,512]{1,0:T(8,128)S(1)}, u32[]{:S(2)}) copy-start(f32[1024,512]{1,0:T(8,128)S(1)} %get-tuple-element.50.lse_ref) | copy-start | bytes 6291460
  236.3 5.8 copy-start.22
  236.3 7.0 slice-start
  243.8 8.5 %copy-start.26 = (bf16[1024,2048]{1,0:T(8,128)(2,1)}, bf16[1024,2048]{1,0:T(8,128)(2,1)S(1)}, u32[]{:S(2)}) copy-start(bf16[1024,2048]{1,0:T(8,128)(2,1)S(1)} %multiply_convert_fusion) | copy-start | bytes 12582916
  395.3 234.2 %all-reduce.8.cloned.1.call-start = ((), (), s32[]{:S(2)}) async-start(), calls=%async_computation.5 | async-start | bytes 67633152 | tf_op jit(solution)/shard_map/psum | solution.py:675
  395.3 6.9 copy-start.25
  395.3 7.1 copy-start.33
  407.3 5.7 copy-start.14
  407.4 6.3 copy-start.16
  407.4 6.5 copy-start.19
  413.9 27.9 %copy-start.42 = (bf16[1024,1376]{1,0:T(8,128)(2,1)S(1)}, bf16[1024,1376]{1,0:T(8,128)(2,1)}, u32[]{:S(2)}) copy-start(bf16[1024,1376]{1,0:T(8,128)(2,1)} %get-tuple-element.48) | copy-start | bytes 8454148
  441.8 8.9 %copy-start.9 = (bf16[1024,512]{1,0:T(8,128)(2,1)}, bf16[1024,512]{1,0:T(8,128)(2,1)S(1)}, u32[]{:S(2)}) copy-start(bf16[1024,512]{1,0:T(8,128)(2,1)S(1)} %get-tuple-element.53.d_q) | copy-start | bytes 3145732
  441.8 8.9 %copy-start.20 = (f32[2048,512]{1,0:T(8,128)}, f32[2048,512]{1,0:T(8,128)S(1)}, u32[]{:S(2)}) copy-start(f32[2048,512]{1,0:T(8,128)S(1)} %get-tuple-element.54.d_k_all) | copy-start | bytes 12582916
  441.8 9.1 %copy-start.21 = (f32[2048,512]{1,0:T(8,128)}, f32[2048,512]{1,0:T(8,128)S(1)}, u32[]{:S(2)}) copy-start(f32[2048,512]{1,0:T(8,128)S(1)} %get-tuple-element.55.d_v_all) | copy-start | bytes 12582916
  441.8 9.1 %copy-start.27 = (bf16[1024,2048]{1,0:T(8,128)(2,1)S(1)}, bf16[1024,2048]{1,0:T(8,128)(2,1)}, u32[]{:S(2)}) copy-start(bf16[1024,2048]{1,0:T(8,128)(2,1)} %copy-done.26) | copy-start | bytes 12582916
  441.8 9.1 %copy-start.41 = (bf16[1024,1376]{1,0:T(8,128)(2,1)S(1)}, bf16[1024,1376]{1,0:T(8,128)(2,1)}, u32[]{:S(2)}) copy-start(bf16[1024,1376]{1,0:T(8,128)(2,1)} %get-tuple-element.88.d_up) | copy-start | bytes 8454148
  450.9 8.8 %copy-start.40 = (bf16[1024,1376]{1,0:T(8,128)(2,1)S(1)}, bf16[1024,1376]{1,0:T(8,128)(2,1)}, u32[]{:S(2)}) copy-start(bf16[1024,1376]{1,0:T(8,128)(2,1)} %get-tuple-element.86.d_gate) | copy-start | bytes 8454148
  476.0 209.0 %all-gather.5.cloned.1.call-start = ((), (), s32[]{:S(2)}) async-start(), calls=%async_computation.3 | async-start | bytes 5242880 | tf_op jit(solution)/shard_map/all_gather | solution.py:681
  608.1 99.8 %all-reduce.6.cloned.1.call-start = ((), (), s32[]{:S(2)}) async-start(), calls=%async_computation.4 | async-start | bytes 33554432 | tf_op jit(solution)/shard_map/psum | solution.py:688
  608.4 7.9 %copy-start.10 = (bf16[1024,512]{1,0:T(8,128)(2,1)S(1)}, bf16[1024,512]{1,0:T(8,128)(2,1)}, u32[]{:S(2)}) copy-start(bf16[1024,512]{1,0:T(8,128)(2,1)} %copy-done.9) | copy-start | bytes 3145732
  608.4 7.9 %copy-start.43 = (bf16[1024,2048]{1,0:T(8,128)(2,1)S(1)}, bf16[1024,2048]{1,0:T(8,128)(2,1)}, u32[]{:S(2)}) copy-start(bf16[1024,2048]{1,0:T(8,128)(2,1)} %get-tuple-element.61) | copy-start | bytes 12582916
  629.5 7.2 copy-start.36
  629.5 7.2 copy-start.37
  641.0 5.8 copy-start.17
  (22 other events, 70.8 us)
Sparse Core Ops, SparseCore 0:
  10.3 49.4 all-gather.2
  395.4 80.5 reduce-scatter.1
  479.9 90.9 all-reduce.7
  608.3 46.6 all-gather.4
  658.1 49.7 all-reduce.5
